TPU v7x, 32 devices: a whole 2x2x4 slice. The times are simulated.
32 devices in a mesh: gx: 4 (over y, x), gy: 4 (over z), gz: 2 (over core).
Axes of the slice: x: 2, y: 2, z: 4, core: 2. Of those that a mesh axis runs over, the one named last changes fastest.
Arguments:
- density: float32 [32, 256, 256], P('gx', 'gy', 'gz'), may hold values from 0.2 to 6, as said below
- momentum: float32 [3, 32, 256, 256], P(None, 'gx', 'gy', 'gz'), may hold values from -6 to 6
- energy: float32 [32, 256, 256], P('gx', 'gy', 'gz'), may hold values from 0.2 to 6, as said below
- displacement: int32 [3, 32, 256, 256], P(None, 'gx', 'gy', 'gz'), may hold values from -255 to 255
- flags: int32 [6], replicated, may hold values from 0 to 1
Outputs:
- new_density: float32 [32, 256, 256], P('gx', 'gy', 'gz')
- new_momentum: float32 [3, 32, 256, 256], P(None, 'gx', 'gy', 'gz')
- new_energy: float32 [32, 256, 256], P('gx', 'gy', 'gz')
- totals: float32 [2], replicated
Inputs may be any that keep to these rules, and one draw needn't show every extreme that they name: density is positive. energy is positive.
All inputs are finite; a program needn't handle non-finite values.
Results may differ from a plain program's by a relative error of at most 0.0003.
Values sent between devices are 32-bit elements; how exact they have to be, the bound alone decides.
A program may use at most 64 MiB of HBM per device.

v0:
```python
import functools

import jax
import jax.numpy as jnp
from jax import lax
from jax.experimental import pallas as pl
from jax.experimental.pallas import tpu as pltpu
from jax.sharding import PartitionSpec as P

AXES = ("gx", "gy", "gz")
SUB = 8


def minmod(p, r):
    return jnp.maximum(jnp.minimum(r, 0.0), jnp.minimum(p, jnp.maximum(r, 0.0)))


def gain(v):
    size = jnp.abs(v)
    return 0.5 * size * (1.0 - size)


def flux(v, g, q_low, q_high, s_low, s_high):
    up = v > 0
    return v * jnp.where(up, q_low, q_high) + g * jnp.where(up, s_low, s_high)


def kernel(
    sizes, flags_in, den, mom, en, disp, out_d, out_m, out_e, sums,
    flags, q, dx, dy, dz, xh, hop, xv, edge, zlo, zhi, cq, cs, sum_x, sum_y, sum_z,
    local_sem, send_sem, recv_sem, ssx, rsx, ssy, rsy, ssz, rsz,
):
    nx, ny, nz = den.shape
    pos = {a: lax.axis_index(a) for a in AXES}
    top = ny + SUB
    per = nz // 4
    parts = edge.shape[0]
    scale = 1.0 / 256.0
    xlo, xhi = xh.at[0], xh.at[1]

    barrier = pltpu.get_barrier_semaphore()
    greeted = 0
    for a in ("gy", "gx", "gz"):
        for o in range(1, sizes[a]):
            peer = lax.rem(pos[a] + o, sizes[a])
            pl.semaphore_signal(
                barrier, inc=1, device_id={a: peer}, device_id_type=pl.DeviceIdType.MESH
            )
            greeted += 1

    locals_ = [
        pltpu.make_async_copy(den, q.at[0, :, SUB:top], local_sem.at[0]),
        pltpu.make_async_copy(mom, q.at[1:4, :, SUB:top], local_sem.at[1]),
        pltpu.make_async_copy(en, q.at[4, :, SUB:top], local_sem.at[2]),
        pltpu.make_async_copy(disp.at[2], dz, local_sem.at[3]),
        pltpu.make_async_copy(disp.at[1], dy.at[:, SUB:top], local_sem.at[4]),
        pltpu.make_async_copy(disp.at[0], dx, local_sem.at[5]),
        pltpu.make_async_copy(flags_in, flags, local_sem.at[6]),
    ]
    for c in locals_:
        c.start()

    pl.semaphore_wait(barrier, greeted)

    def copy(k, src, dst, axis, step):
        return pltpu.make_async_remote_copy(
            src_ref=src, dst_ref=dst, send_sem=send_sem.at[k], recv_sem=recv_sem.at[k],
            device_id={axis: pos[axis] + step}, device_id_type=pl.DeviceIdType.MESH,
        )

    last = {a: sizes[a] - 1 for a in AXES}
    me = pos["gx"]
    par = lax.rem(me, 2)
    odd = par == 1
    end = last["gx"]
    leg_out = (odd & (me + 2 <= end)) | ((par == 0) & (me >= 2))
    relays = (odd & (me >= 3)) | ((par == 0) & (me + 2 <= end))
    leg_in = (me + 1 <= end) & (odd | (me >= 2))
    begin = par * (nx - 2)
    other = 1 - par

    def remote(k, src, dst, target):
        return pltpu.make_async_remote_copy(
            src_ref=src, dst_ref=dst, send_sem=send_sem.at[k], recv_sem=recv_sem.at[k],
            device_id={"gx": target}, device_id_type=pl.DeviceIdType.MESH,
        )

    over = me + 4 * par - 2
    legs = [
        remote(16, mom.at[0, pl.ds(begin, 2)], hop.at[0:2], over),
        remote(17, mom.at[1, pl.ds(begin, 2)], hop.at[2:4], over),
        remote(18, en.at[begin], hop.at[4], over),
    ]
    beside = me + 1 - 2 * par
    onward = [
        remote(19, hop.at[0:2], xh.at[other, 1], beside),
        remote(20, hop.at[2:4], xh.at[other, 2], beside),
        remote(21, hop.at[4], xh.at[other, 4, 0], beside),
    ]
    landed = [
        remote(19, hop.at[0:2], xh.at[par, 1], beside),
        remote(20, hop.at[2:4], xh.at[par, 2], beside),
        remote(21, hop.at[4], xh.at[par, 4, 0], beside),
    ]
    x_up = [
        copy(0, den.at[nx - 2 : nx], xlo.at[0], "gx", 1),
        copy(1, mom.at[2, nx - 2 : nx], xlo.at[3], "gx", 1),
        copy(2, en.at[nx - 1], xlo.at[4, 1], "gx", 1),
    ]
    x_up_half = [
        copy(22, mom.at[0:2, nx - 2 : nx], xlo.at[1:3], "gx", 1),
        copy(23, en.at[nx - 2], xlo.at[4, 0], "gx", 1),
    ]
    x_down = [
        copy(6, disp.at[0, 0], xv, "gx", -1),
        copy(3, den.at[0:2], xhi.at[0], "gx", -1),
        copy(4, mom.at[2, 0:2], xhi.at[3], "gx", -1),
        copy(5, en.at[1], xhi.at[4, 1], "gx", -1),
    ]
    x_down_half = [
        copy(24, mom.at[0:2, 0:2], xhi.at[1:3], "gx", -1),
        copy(25, en.at[0], xhi.at[4, 0], "gx", -1),
    ]
    up_half = (me < end) & ~(leg_out & odd)
    down_half = (me > 0) & ~(leg_out & (par == 0))
    low_half = (me > 0) & ~(leg_in & (par == 0))
    high_half = (me < end) & ~(leg_in & odd)

    def each(cond, copies, act):
        @pl.when(cond)
        def _():
            for c in copies:
                act(c)

    def go(c):
        c.start()

    hi_rows = slice(top, top + SUB)
    y_up = [
        copy(7, den.at[:, ny - SUB : ny], q.at[0, :, 0:SUB], "gy", 1),
        copy(8, mom.at[:, :, ny - SUB : ny], q.at[1:4, :, 0:SUB], "gy", 1),
        copy(9, en.at[:, ny - SUB : ny], q.at[4, :, 0:SUB], "gy", 1),
    ]
    y_down = [
        copy(10, den.at[:, 0:SUB], q.at[0, :, hi_rows], "gy", -1),
        copy(11, mom.at[:, :, 0:SUB], q.at[1:4, :, hi_rows], "gy", -1),
        copy(12, en.at[:, 0:SUB], q.at[4, :, hi_rows], "gy", -1),
        copy(13, disp.at[1, :, 0:SUB], dy.at[:, hi_rows], "gy", -1),
    ]
    z_up = [copy(14, edge, zlo, "gz", 1)]
    z_down = [copy(15, edge, zhi, "gz", -1)]

    def start(axis, ups, downs):
        @pl.when(pos[axis] < last[axis])
        def _():
            for c in ups:
                c.start()

        @pl.when(pos[axis] > 0)
        def _():
            for c in downs:
                c.start()

    def arrive(axis, ups, downs, fill_low, fill_high):
        @pl.when(pos[axis] > 0)
        def _():
            for c in ups:
                c.wait_recv()

        @pl.when(pos[axis] < last[axis])
        def _():
            for c in downs:
                c.wait_recv()

        @pl.when(pos[axis] == 0)
        def _():
            fill_low()

        @pl.when(pos[axis] == last[axis])
        def _():
            fill_high()

    def sent(axis, ups, downs):
        @pl.when(pos[axis] < last[axis])
        def _():
            for c in ups:
                c.wait_send()

        @pl.when(pos[axis] > 0)
        def _():
            for c in downs:
                c.wait_send()

    each(leg_out, legs, go)
    each(odd & (me < end), x_up, go)
    each(me > 0, x_down, go)
    each((par == 0) & (me < end), x_up, go)
    each(up_half, x_up_half, go)
    each(down_half, x_down_half, go)
    start("gy", y_up, y_down)

    for c in locals_:
        c.wait()

    flag = [flags[i].astype(jnp.float32) for i in range(6)]

    def low_mult(a):
        return jnp.where(pos[AXES[a]] == 0, flag[2 * a], 1.0)

    def high_mult(a):
        return jnp.where(pos[AXES[a]] == last[AXES[a]], flag[2 * a + 1], 1.0)

    def outer_low(a):
        return jnp.where(pos[AXES[a]] == 0, flag[2 * a], 0.0)

    def outer_high(a):
        return jnp.where(pos[AXES[a]] == last[AXES[a]], flag[2 * a + 1], 0.0)

    lane = lax.broadcasted_iota(jnp.int32, (ny, nz), 1)
    row = lax.broadcasted_iota(jnp.int32, (ny, nz), 0)

    def pack(x, carry):
        new = list(carry)
        for f in range(6):
            p = f * nx + x
            k = f * nx // per
            at = 4 * lax.rem(p, per)
            plane = q[f, x, SUB:top] if f < 5 else dz[x].astype(jnp.float32)
            moved = pltpu.roll(plane, at, 1)
            mine = lax.rem(lane + 2 - at + nz, nz) < 4
            new[k] = jnp.where(mine, moved, new[k])
        return tuple(new)

    packed = lax.fori_loop(0, nx, pack, tuple(jnp.zeros((ny, nz), jnp.float32) for _ in range(parts)))
    for k in range(parts):
        edge[k] = packed[k]

    wz = jnp.where(lane == 0, outer_low(2), 0.0) - jnp.where(lane == nz - 1, outer_high(2), 0.0)
    wy = jnp.where(row == 0, outer_low(1), 0.0) - jnp.where(row == ny - 1, outer_high(1), 0.0)
    wx_low, wx_high = outer_low(0), outer_high(0)

    def total(x, carry):
        a, b = carry
        wx = jnp.where(x == 0, wx_low, 0.0) - jnp.where(x == nx - 1, wx_high, 0.0)
        w = 1.0 + scale * (
            wz * dz[x].astype(jnp.float32)
            + wy * dy[x, SUB:top].astype(jnp.float32)
            + wx * dx[x].astype(jnp.float32)
        )
        return (
            a + jnp.sum((q[0, x, SUB:top] * w).reshape(ny // SUB, SUB, nz), 0),
            b + jnp.sum((q[4, x, SUB:top] * w).reshape(ny // SUB, SUB, nz), 0),
        )

    zero = jnp.zeros((SUB, nz), jnp.float32)
    mass, power = lax.fori_loop(0, nx, total, (zero, zero))
    sum_z[pos["gz"], 0] = mass
    sum_z[pos["gz"], 1] = power
    start("gz", z_up, z_down)

    def line(axis, slots, ss, rs):
        count = sizes[axis]
        copies = []
        for o in range(1, count):
            me = pos[axis]
            copies.append(
                pltpu.make_async_remote_copy(
                    src_ref=slots.at[me], dst_ref=slots.at[me], send_sem=ss.at[o],
                    recv_sem=rs.at[me], device_id={axis: lax.rem(me + o, count)},
                    device_id_type=pl.DeviceIdType.MESH,
                )
            )
        return copies

    def collect(axis, slots, ss, rs):
        count = sizes[axis]
        for o in range(1, count):
            peer = lax.rem(pos[axis] + o, count)
            pltpu.make_async_remote_copy(
                src_ref=slots.at[peer], dst_ref=slots.at[peer], send_sem=ss.at[o],
                recv_sem=rs.at[peer], device_id={axis: peer},
                device_id_type=pl.DeviceIdType.MESH,
            ).wait_recv()
        a, b = slots[0, 0], slots[0, 1]
        for o in range(1, count):
            a = a + slots[o, 0]
            b = b + slots[o, 1]
        return a, b

    line_z = line("gz", sum_z, ssz, rsz)
    line_y = line("gy", sum_y, ssy, rsy)
    line_x = line("gx", sum_x, ssx, rsx)
    for c in line_z:
        c.start()

    def z_low():
        e = edge[...]
        zlo[...] = jnp.where(lane3 & 3 == 3, pltpu.roll(e, nz - 1, 2), pltpu.roll(e, nz - 2, 2))

    def z_high():
        e = edge[...]
        zhi[...] = jnp.where(lane3 & 3 == 0, pltpu.roll(e, 1, 2), pltpu.roll(e, 2, 2))

    lane3 = lax.broadcasted_iota(jnp.int32, (parts, ny, nz), 2)
    arrive("gz", z_up, z_down, z_low, z_high)
    low = lane & 3 == 0
    for k in range(parts):
        e, l, h = edge[k], zlo[k], zhi[k]
        r1, r2 = pltpu.roll(l, 1, 1), pltpu.roll(l, 2, 1)
        l1, l2 = pltpu.roll(h, nz - 1, 1), pltpu.roll(h, nz - 2, 1)
        cq[k] = jnp.where(low, r1, l1)
        cs[k] = jnp.where(low, minmod(e - r1, r1 - r2), minmod(l2 - l1, l1 - e))

    first, final = lane == 0, lane == nz - 1
    z_lo_mult = jnp.where(first, low_mult(2), 1.0) * scale
    z_hi_mult = high_mult(2) * scale
    outs = (
        lambda x: out_d.at[x], lambda x: out_m.at[0, x], lambda x: out_m.at[1, x],
        lambda x: out_m.at[2, x], lambda x: out_e.at[x],
    )

    def along_z(x, _):
        v = dz[x].astype(jnp.float32) * z_lo_mult
        g = gain(v)

        def ghosts(ref, f):
            back = lax.rem(nz - 4 * lax.rem(f * nx + x, per), nz)
            return pltpu.roll(ref[f * nx // per], back, 1)

        vh = ghosts(cq, 5) * z_hi_mult
        gh = gain(vh)
        for f in range(5):
            plane = q[f, x, SUB:top]
            gq, gs = ghosts(cq, f), ghosts(cs, f)
            qm = jnp.where(first, gq, pltpu.roll(plane, 1, 1))
            d = plane - qm
            s = minmod(jnp.where(final, gq - plane, pltpu.roll(d, nz - 1, 1)), d)
            sm = jnp.where(first, gs, pltpu.roll(s, 1, 1))
            fl = flux(v, g, qm, plane, sm, s)
            fh = jnp.where(final, flux(vh, gh, plane, gq, s, gs), pltpu.roll(fl, nz - 1, 1))
            outs[f](x)[...] = plane + (fl - fh)
        return 0

    lax.fori_loop(0, nx, along_z, 0)

    @pl.when(relays)
    def _():
        for a, b in zip(legs, onward):
            a.wait_recv()
            b.start()

    a, b = collect("gz", sum_z, ssz, rsz)
    sum_y[pos["gy"], 0] = a
    sum_y[pos["gy"], 1] = b

    def y_low():
        q[:, :, 0:SUB] = jnp.broadcast_to(q[:, :, SUB : SUB + 1], (5, nx, SUB, nz))

    def y_high():
        q[:, :, hi_rows] = jnp.broadcast_to(q[:, :, top - 1 : top], (5, nx, SUB, nz))
        dy[:, hi_rows] = jnp.broadcast_to(dy[:, top - 1 : top], (nx, SUB, nz))

    arrive("gy", y_up, y_down, y_low, y_high)
    for c in line_y:
        c.start()
    tall = ny + 2 * SUB
    rows = lax.broadcasted_iota(jnp.int32, (tall, nz), 0)
    inside = (rows >= SUB) & (rows <= top)
    y_mult = jnp.where(
        rows == SUB, low_mult(1) * scale, jnp.where(rows == top, high_mult(1) * scale, scale)
    )

    def along_y(x, _):
        v = jnp.where(inside, dy[x].astype(jnp.float32), 0.0) * y_mult
        g = gain(v)
        for f in range(5):
            plane = q[f, x]
            qm = pltpu.roll(plane, 1, 0)
            d = plane - qm
            s = minmod(pltpu.roll(d, tall - 1, 0), d)
            fl = flux(v, g, qm, plane, pltpu.roll(s, 1, 0), s)
            ch = fl - pltpu.roll(fl, tall - 1, 0)
            outs[f](x)[...] += ch[SUB:top]
        return 0

    lax.fori_loop(0, nx, along_y, 0)

    a, b = collect("gy", sum_y, ssy, rsy)
    sum_x[pos["gx"], 0] = a
    sum_x[pos["gx"], 1] = b

    def core(r, _):
        at = pl.ds(pl.multiple_of(r * SUB, SUB), SUB)
        inner = pl.ds(pl.multiple_of(r * SUB + SUB, SUB), SUB)
        vs = [dx[c, at].astype(jnp.float32) * scale for c in range(2, nx - 1)]
        gs = [gain(v) for v in vs]
        for f in range(5):
            line_q = [q[f, c, inner] for c in range(nx)]
            ds = [line_q[i + 1] - line_q[i] for i in range(nx - 1)]
            ss = [minmod(ds[i + 1], ds[i]) for i in range(nx - 2)]
            fl = [
                flux(vs[i], gs[i], line_q[i + 1], line_q[i + 2], ss[i], ss[i + 1])
                for i in range(nx - 3)
            ]
            for c in range(1, nx - 1):
                change = fl[c - 2] if c >= 2 else 0.0
                ref = outs[f](c)
                ref[at] += change - fl[c - 1] if c < nx - 2 else change
        return 0

    lax.fori_loop(0, ny // SUB, core, 0)

    def x_low():
        xlo[...] = jnp.broadcast_to(q[:, 0:1, SUB:top], (5, 2, ny, nz))

    def x_high():
        xhi[...] = jnp.broadcast_to(q[:, nx - 1 : nx, SUB:top], (5, 2, ny, nz))
        xv[...] = dx[nx - 1]

    for c in line_x:
        c.start()
    arrive("gx", x_up, x_down, x_low, x_high)
    x_lo_mult, x_hi_mult = low_mult(0) * scale, high_mult(0) * scale

    def x_rows(r):
        return pl.ds(pl.multiple_of(r * SUB, SUB), SUB), pl.ds(
            pl.multiple_of(r * SUB + SUB, SUB), SUB
        )

    def x_flux(v, g, cells4):
        ds = [cells4[i + 1] - cells4[i] for i in range(3)]
        return flux(
            v, g, cells4[1], cells4[2], minmod(ds[1], ds[0]), minmod(ds[2], ds[1])
        )

    def rim(fields, r, _):
        at, inner = x_rows(r)
        faces = (0, 1, nx - 1, nx)
        vs = [
            dx[0, at].astype(jnp.float32) * x_lo_mult,
            dx[1, at].astype(jnp.float32) * scale,
            dx[nx - 1, at].astype(jnp.float32) * scale,
            xv[at].astype(jnp.float32) * x_hi_mult,
        ]
        gs = [gain(v) for v in vs]
        for f in fields:
            a = [xlo[f, 0, at], xlo[f, 1, at]] + [q[f, c, inner] for c in range(3)]
            b = [q[f, c, inner] for c in range(nx - 3, nx)] + [xhi[f, 0, at], xhi[f, 1, at]]
            fl = [x_flux(vs[i], gs[i], (a, a, b, b)[i][i % 2 : i % 2 + 4]) for i in range(4)]
            for c, change in (
                (0, fl[0] - fl[1]), (1, fl[1]), (nx - 2, -fl[2]), (nx - 1, fl[2] - fl[3]),
            ):
                ref = outs[f](c)
                ref[at] += change
        return 0

    lax.fori_loop(0, ny // SUB, functools.partial(rim, (0, 3)), 0)
    for part, whole, fields in ((0, (0,), (1,)), (1, (), (2,)), (2, (1,), (4,))):
        each(low_half, [x_up_half[k] for k in whole], lambda c: c.wait_recv())
        each(high_half, [x_down_half[k] for k in whole], lambda c: c.wait_recv())
        each(leg_in, landed[part : part + 1], lambda c: c.wait_recv())
        lax.fori_loop(0, ny // SUB, functools.partial(rim, fields), 0)

    a, b = collect("gx", sum_x, ssx, rsx)
    sums[0] = a
    sums[1] = b
    sent("gx", x_up, x_down)
    each(leg_out, legs, lambda c: c.wait_send())
    each(relays, onward, lambda c: c.wait_send())
    each(up_half, x_up_half, lambda c: c.wait_send())
    each(down_half, x_down_half, lambda c: c.wait_send())
    sent("gy", y_up, y_down)
    sent("gz", z_up, z_down)
    for c in line_x + line_y + line_z:
        c.wait_send()


def put(cells, den, mom, en, sums, out_d, out_m, out_e, totals, sem):
    pairs = ((mom, out_m), (den, out_d), (en, out_e))
    moves = [
        pltpu.make_async_copy(src, dst, sem.at[i]) for i, (src, dst) in enumerate(pairs)
    ]
    for c in moves:
        c.start()
    totals[0] = jnp.sum(sums[0]) / cells
    totals[1] = jnp.sum(sums[1]) / cells
    for c in moves:
        c.wait()


def shards(density, momentum, energy, displacement, flags):
    sizes = {a: lax.axis_size(a) for a in AXES}
    nx, ny, nz = density.shape
    tall = ny + 2 * SUB
    per = nz // 4
    parts = -(-6 * nx // per)
    f32, i32 = jnp.float32, jnp.int32
    dma = pltpu.SemaphoreType.DMA
    any_ = pl.BlockSpec(memory_space=pl.ANY)
    hbm = pl.BlockSpec(memory_space=pltpu.HBM)
    vmem = pl.BlockSpec(memory_space=pltpu.VMEM)
    smem = pl.BlockSpec(memory_space=pltpu.SMEM)
    cells = float(nx * ny * nz)
    for a in AXES:
        cells = cells * sizes[a]
    outputs = tuple(jax.ShapeDtypeStruct(v.shape, f32) for v in (density, momentum, energy))
    results = pl.pallas_call(
        functools.partial(kernel, sizes),
        out_shape=outputs + (jax.ShapeDtypeStruct((2, SUB, nz), f32),),
        in_specs=[hbm] * 5,
        out_specs=(vmem, vmem, vmem, vmem),
        scratch_shapes=[
            pltpu.SMEM((6,), i32),
            pltpu.VMEM((5, nx, tall, nz), f32),
            pltpu.VMEM((nx, ny, nz), i32),
            pltpu.VMEM((nx, tall, nz), i32),
            pltpu.VMEM((nx, ny, nz), i32),
            pltpu.VMEM((2, 5, 2, ny, nz), f32),
            pltpu.VMEM((5, ny, nz), f32),
            pltpu.VMEM((ny, nz), i32),
        ]
        + [pltpu.VMEM((parts, ny, nz), f32) for _ in range(5)]
        + [pltpu.VMEM((sizes[a], 2, SUB, nz), f32) for a in AXES]
        + [dma((7,)), dma((26,)), dma((26,))]
        + [dma((sizes[a],)) for a in AXES for _ in range(2)],
        compiler_params=pltpu.CompilerParams(
            collective_id=0, has_side_effects=True, vmem_limit_bytes=12 << 20
        ),
    )(
        *(
            pltpu.with_memory_space_constraint(v, pltpu.HBM)
            for v in (flags, density, momentum, energy, displacement)
        )
    )
    return pl.pallas_call(
        functools.partial(put, cells),
        out_shape=outputs + (jax.ShapeDtypeStruct((2,), f32),),
        in_specs=[any_, any_, any_, vmem],
        out_specs=(hbm, hbm, hbm, smem),
        scratch_shapes=[dma((3,))],
        compiler_params=pltpu.CompilerParams(vmem_limit_bytes=2 << 20),
    )(*results)


def solution(mesh):
    return jax.shard_map(
        shards,
        mesh=mesh,
        in_specs=(
            P("gx", "gy", "gz"),
            P(None, "gx", "gy", "gz"),
            P("gx", "gy", "gz"),
            P(None, "gx", "gy", "gz"),
            P(),
        ),
        out_specs=(P("gx", "gy", "gz"), P(None, "gx", "gy", "gz"), P("gx", "gy", "gz"), P()),
        check_vma=False,
    )
```

profile of v0, /device:TPU:0, one launch (start us, length us, event | category | flops | bytes accessed | tf_op | source)
XLA Modules:
  0.0 22.7 jit_solution(1112613870383898788)
XLA Ops:
  0.6 20.4 %shard_map.84 = (f32[8,64,128]{2,1,0:T(8,128)S(1)}, f32[3,8,64,128]{3,2,1,0:T(8,128)S(1)}, f32[8,64,128]{2,1,0:T(8,128)S(1)}, f32[2,8,128]{2,1,0:T(8,128)S(1)}) custom-call(s32[6]{0:T(128)} %flags_in.1, f32[8,64,128]{2,1,0:T(8,128)} %den.1, f32[3,8,64,128]{3,2,1,0:T(8,128)} %mom.1, f32[8,64,128]{2,1,0:T(8,128)} %en.1, s32[3,8,64,128]{3,2,1,0:T(8,128)} %disp.1), custom_call_target="tpu_custom_call" | custom-call | tf_op jit(solution)/shard_map/pallas_call | solution.py:507
  21.1 1.6 %shard_map.85 = (f32[8,64,128]{2,1,0:T(8,128)}, f32[3,8,64,128]{3,2,1,0:T(8,128)}, f32[8,64,128]{2,1,0:T(8,128)}, f32[2]{0:T(128)}) custom-call(f32[8,64,128]{2,1,0:T(8,128)S(1)} %get-tuple-element.8.den, f32[3,8,64,128]{3,2,1,0:T(8,128)S(1)} %get-tuple-element.9.mom, f32[8,64,128]{2,1,0:T(8,128)S(1)} %get-tuple-element.10.en, ...), custom_call_target="tpu_custom_call" | custom-call | tf_op jit(solution)/shard_map/pallas_call | solution.py:535
where the time goes:
time: 22.8 us; the launch traced here: 22.7 us
  Pallas kernels  22 us (96%)
  between operations  0.64 us (3%)
    pallas_call x1, Pallas kernels, shards(): pl.pallas_call(functools.partial(kernel, sizes), out_shape=outputs + (jax...  20.4 us
    pallas_call x1, Pallas kernels, shards(): pl.pallas_call(functools.partial(put, cells), out_shape=outputs + (jax.Sh...  1.59 us

commit v1 on v0

v1 whole, which is shorter than its diff:
```python
import functools

import jax
import jax.numpy as jnp
from jax import lax
from jax.experimental import pallas as pl
from jax.experimental.pallas import tpu as pltpu
from jax.sharding import PartitionSpec as P

AXES = ("gx", "gy", "gz")
SUB = 8


def minmod(p, r):
    return jnp.maximum(jnp.minimum(r, 0.0), jnp.minimum(p, jnp.maximum(r, 0.0)))


def gain(v):
    size = jnp.abs(v)
    return 0.5 * size * (1.0 - size)


def flux(v, g, q_low, q_high, s_low, s_high):
    up = v > 0
    return v * jnp.where(up, q_low, q_high) + g * jnp.where(up, s_low, s_high)


def kernel(
    sizes, flags_in, den, mom, en, disp, out_d, out_m, out_e, sums,
    flags, q, dx, dy, dz, xh, hop, xv, edge, zlo, zhi, cq, cs, part, slots, done,
    local_sem, send_sem, recv_sem, in_sem, sum_send, sum_recv,
):
    nx, ny, nz = den.shape
    pos = {a: lax.axis_index(a) for a in AXES}
    last = {a: sizes[a] - 1 for a in AXES}
    top = ny + SUB
    per = nz // 4
    parts = edge.shape[0]
    scale = 1.0 / 256.0
    xlo, xhi = xh.at[0], xh.at[1]
    own = slice(SUB, top)
    mesh_ids = pl.DeviceIdType.MESH

    locals_ = [
        pltpu.make_async_copy(flags_in, flags, local_sem.at[6]),
        pltpu.make_async_copy(den, q.at[0, :, own], local_sem.at[0]),
        pltpu.make_async_copy(en, q.at[4, :, own], local_sem.at[2]),
        pltpu.make_async_copy(disp.at[2], dz, local_sem.at[3]),
        pltpu.make_async_copy(disp.at[1], dy.at[:, own], local_sem.at[4]),
        pltpu.make_async_copy(disp.at[0], dx, local_sem.at[5]),
        pltpu.make_async_copy(mom, q.at[1:4, :, own], local_sem.at[1]),
    ]
    for c in locals_:
        c.start()

    me = pos["gx"]
    par = lax.rem(me, 2)
    odd = par == 1
    end = last["gx"]
    reach = [("gx", 1, 0, me > 0), ("gx", 2, 1, odd), ("gy", 1, 2, True), ("gz", 1, 3, True)]

    barrier = pltpu.get_barrier_semaphore()
    below = sum(jnp.where(pos[a] >= o, 1, 0) for a, o, _, _ in reach)

    @pl.when(below > 0)
    def _():
        pl.semaphore_wait(barrier, below)

    for a, o, k, told in reach:
        @pl.when(pos[a] + o <= last[a])
        def _(a=a, o=o):
            pl.semaphore_signal(
                barrier, inc=1, device_id={a: pos[a] + o}, device_id_type=mesh_ids
            )

        @pl.when((pos[a] >= o) & told)
        def _(a=a, o=o, k=k):
            pl.semaphore_signal(
                in_sem.at[k], inc=1, device_id={a: pos[a] - o}, device_id_type=mesh_ids
            )

    def is_in(a, o, k, cond=True):
        @pl.when((pos[a] + o <= last[a]) & cond)
        def _():
            pl.semaphore_wait(in_sem.at[k], 1)

    def copy(k, src, dst, axis, step):
        return pltpu.make_async_remote_copy(
            src_ref=src, dst_ref=dst, send_sem=send_sem.at[k], recv_sem=recv_sem.at[k],
            device_id={axis: pos[axis] + step}, device_id_type=mesh_ids,
        )

    leg_up = odd & (me + 2 <= end)
    leg_down = (par == 0) & (me >= 2)
    leg_out = leg_up | leg_down
    relays = (odd & (me >= 3)) | ((par == 0) & (me + 2 <= end))
    leg_in = (me + 1 <= end) & (odd | (me >= 2))
    other = 1 - par

    legs_up = [
        copy(16, q.at[1, nx - 2 : nx, own], hop.at[0:2], "gx", 2),
        copy(17, q.at[2, nx - 2 : nx, own], hop.at[2:4], "gx", 2),
        copy(18, q.at[4, nx - 2, own], hop.at[4], "gx", 2),
    ]
    legs_down = [
        copy(16, mom.at[0, 0:2], hop.at[0:2], "gx", -2),
        copy(17, mom.at[1, 0:2], hop.at[2:4], "gx", -2),
        copy(18, en.at[0], hop.at[4], "gx", -2),
    ]
    beside = 1 - 2 * par
    onward = [
        copy(19, hop.at[0:2], xh.at[other, 1], "gx", beside),
        copy(20, hop.at[2:4], xh.at[other, 2], "gx", beside),
        copy(21, hop.at[4], xh.at[other, 4, 0], "gx", beside),
    ]
    landed = [
        copy(19, hop.at[0:2], xh.at[par, 1], "gx", beside),
        copy(20, hop.at[2:4], xh.at[par, 2], "gx", beside),
        copy(21, hop.at[4], xh.at[par, 4, 0], "gx", beside),
    ]
    x_up = [
        copy(0, q.at[0, nx - 2 : nx, own], xlo.at[0], "gx", 1),
        copy(1, q.at[3, nx - 2 : nx, own], xlo.at[3], "gx", 1),
        copy(2, q.at[4, nx - 1, own], xlo.at[4, 1], "gx", 1),
    ]
    x_up_half = [
        copy(22, q.at[1:3, nx - 2 : nx, own], xlo.at[1:3], "gx", 1),
        copy(23, q.at[4, nx - 2, own], xlo.at[4, 0], "gx", 1),
    ]
    x_down = [
        copy(6, disp.at[0, 0], xv, "gx", -1),
        copy(3, den.at[0:2], xhi.at[0], "gx", -1),
        copy(4, mom.at[2, 0:2], xhi.at[3], "gx", -1),
        copy(5, en.at[1], xhi.at[4, 1], "gx", -1),
    ]
    x_down_half = [
        copy(24, mom.at[0:2, 0:2], xhi.at[1:3], "gx", -1),
        copy(25, en.at[0], xhi.at[4, 0], "gx", -1),
    ]
    up_half = (me < end) & ~leg_up
    down_half = (me > 0) & ~leg_down
    low_half = (me > 0) & ~(leg_in & (par == 0))
    high_half = (me < end) & ~(leg_in & odd)

    def each(cond, copies, act):
        @pl.when(cond)
        def _():
            for c in copies:
                act(c)

    def go(c):
        c.start()

    hi_rows = slice(top, top + SUB)
    y_up = [
        copy(7, q.at[0, :, ny:top], q.at[0, :, 0:SUB], "gy", 1),
        copy(8, q.at[1:4, :, ny:top], q.at[1:4, :, 0:SUB], "gy", 1),
        copy(9, q.at[4, :, ny:top], q.at[4, :, 0:SUB], "gy", 1),
    ]
    y_down = [
        copy(10, den.at[:, 0:SUB], q.at[0, :, hi_rows], "gy", -1),
        copy(11, mom.at[:, :, 0:SUB], q.at[1:4, :, hi_rows], "gy", -1),
        copy(12, en.at[:, 0:SUB], q.at[4, :, hi_rows], "gy", -1),
        copy(13, disp.at[1, :, 0:SUB], dy.at[:, hi_rows], "gy", -1),
    ]
    z_up = [copy(14, edge, zlo, "gz", 1)]
    z_down = [copy(15, edge, zhi, "gz", -1)]

    def arrive(axis, ups, downs, fill_low, fill_high):
        @pl.when(pos[axis] > 0)
        def _():
            for c in ups:
                c.wait_recv()

        @pl.when(pos[axis] < last[axis])
        def _():
            for c in downs:
                c.wait_recv()

        @pl.when(pos[axis] == 0)
        def _():
            fill_low()

        @pl.when(pos[axis] == last[axis])
        def _():
            fill_high()

    def sent(axis, ups, downs):
        @pl.when(pos[axis] < last[axis])
        def _():
            for c in ups:
                c.wait_send()

        @pl.when(pos[axis] > 0)
        def _():
            for c in downs:
                c.wait_send()

    below_x, below_y, below_z = me > 0, pos["gy"] > 0, pos["gz"] > 0
    above_x, above_y, above_z = (pos[a] < last[a] for a in AXES)
    each(leg_down, legs_down, go)
    each(below_x, x_down, go)
    each(down_half, x_down_half, go)
    each(below_y, y_down, go)

    for c in locals_[:-1]:
        c.wait()

    flag = [flags[i].astype(jnp.float32) for i in range(6)]

    def low_mult(a):
        return jnp.where(pos[AXES[a]] == 0, flag[2 * a], 1.0)

    def high_mult(a):
        return jnp.where(pos[AXES[a]] == last[AXES[a]], flag[2 * a + 1], 1.0)

    def outer_low(a):
        return jnp.where(pos[AXES[a]] == 0, flag[2 * a], 0.0)

    def outer_high(a):
        return jnp.where(pos[AXES[a]] == last[AXES[a]], flag[2 * a + 1], 0.0)

    lane = lax.broadcasted_iota(jnp.int32, (ny, nz), 1)
    row = lax.broadcasted_iota(jnp.int32, (ny, nz), 0)
    wz = jnp.where(lane == 0, outer_low(2), 0.0) - jnp.where(lane == nz - 1, outer_high(2), 0.0)
    wy = jnp.where(row == 0, outer_low(1), 0.0) - jnp.where(row == ny - 1, outer_high(1), 0.0)
    wx_low, wx_high = outer_low(0), outer_high(0)

    def total(x, carry):
        a, b = carry
        wx = jnp.where(x == 0, wx_low, 0.0) - jnp.where(x == nx - 1, wx_high, 0.0)
        w = 1.0 + scale * (
            wz * dz[x].astype(jnp.float32)
            + wy * dy[x, own].astype(jnp.float32)
            + wx * dx[x].astype(jnp.float32)
        )
        return (
            a + jnp.sum((q[0, x, own] * w).reshape(ny // SUB, SUB, nz), 0),
            b + jnp.sum((q[4, x, own] * w).reshape(ny // SUB, SUB, nz), 0),
        )

    zero = jnp.zeros((SUB, nz), jnp.float32)
    mass, power = lax.fori_loop(0, nx, total, (zero, zero))
    part[0:1] = jnp.sum(mass, 0, keepdims=True)
    part[1:2] = jnp.sum(power, 0, keepdims=True)

    sx, sy, sz = (sizes[a] for a in AXES)
    count = sx * sy * sz
    index = (pos["gx"] * sy + pos["gy"]) * sz + pos["gz"]
    first_device = index == 0

    def place(i):
        return {"gx": i // (sy * sz), "gy": i // sz % sy, "gz": i % sz}

    def message(src, dst, k, target):
        return pltpu.make_async_remote_copy(
            src_ref=src, dst_ref=dst, send_sem=sum_send.at[k], recv_sem=sum_recv.at[k],
            device_id=target, device_id_type=mesh_ids,
        )

    away = place(count - 1)
    inward = message(part, slots.at[index], 0, place(0))
    gathered = message(slots.at[1:count], slots.at[1:count], 0, away)
    outward = message(done, done, 1, place(0))
    scattered = message(slots.at[1:count], slots.at[1:count], 1, away)

    @pl.when(~first_device)
    def _():
        inward.start()

    locals_[-1].wait()

    def pack(x, carry):
        new = list(carry)
        for f in range(6):
            p = f * nx + x
            k = f * nx // per
            at = 4 * lax.rem(p, per)
            plane = q[f, x, own] if f < 5 else dz[x].astype(jnp.float32)
            moved = pltpu.roll(plane, at, 1)
            mine = lax.rem(lane + 2 - at + nz, nz) < 4
            new[k] = jnp.where(mine, moved, new[k])
        return tuple(new)

    packed = lax.fori_loop(0, nx, pack, tuple(jnp.zeros((ny, nz), jnp.float32) for _ in range(parts)))
    for k in range(parts):
        edge[k] = packed[k]
    each(below_z, z_down, go)
    is_in("gz", 1, 3)
    each(above_z, z_up, go)
    is_in("gx", 1, 0, me + 1 > 0)
    each(above_x, x_up, go)
    each(up_half, x_up_half, go)
    is_in("gx", 2, 1, odd)
    each(leg_up, legs_up, go)
    is_in("gy", 1, 2)
    each(above_y, y_up, go)

    outs = (
        lambda x: out_d.at[x], lambda x: out_m.at[0, x], lambda x: out_m.at[1, x],
        lambda x: out_m.at[2, x], lambda x: out_e.at[x],
    )

    def core(r, _):
        at = pl.ds(pl.multiple_of(r * SUB, SUB), SUB)
        inner = pl.ds(pl.multiple_of(r * SUB + SUB, SUB), SUB)
        vs = [dx[c, at].astype(jnp.float32) * scale for c in range(2, nx - 1)]
        gs = [gain(v) for v in vs]
        for f in range(5):
            line_q = [q[f, c, inner] for c in range(nx)]
            ds = [line_q[i + 1] - line_q[i] for i in range(nx - 1)]
            ss = [minmod(ds[i + 1], ds[i]) for i in range(nx - 2)]
            fl = [
                flux(vs[i], gs[i], line_q[i + 1], line_q[i + 2], ss[i], ss[i + 1])
                for i in range(nx - 3)
            ]
            for c in range(nx):
                new = line_q[c]
                if 2 <= c < nx - 1:
                    new = new + fl[c - 2]
                if 1 <= c < nx - 2:
                    new = new - fl[c - 1]
                outs[f](c)[at] = new
        return 0

    lax.fori_loop(0, ny // SUB, core, 0)

    def z_low():
        e = edge[...]
        zlo[...] = jnp.where(lane3 & 3 == 3, pltpu.roll(e, nz - 1, 2), pltpu.roll(e, nz - 2, 2))

    def z_high():
        e = edge[...]
        zhi[...] = jnp.where(lane3 & 3 == 0, pltpu.roll(e, 1, 2), pltpu.roll(e, 2, 2))

    lane3 = lax.broadcasted_iota(jnp.int32, (parts, ny, nz), 2)
    arrive("gz", z_up, z_down, z_low, z_high)
    low = lane & 3 == 0
    for k in range(parts):
        e, l, h = edge[k], zlo[k], zhi[k]
        r1, r2 = pltpu.roll(l, 1, 1), pltpu.roll(l, 2, 1)
        l1, l2 = pltpu.roll(h, nz - 1, 1), pltpu.roll(h, nz - 2, 1)
        cq[k] = jnp.where(low, r1, l1)
        cs[k] = jnp.where(low, minmod(e - r1, r1 - r2), minmod(l2 - l1, l1 - e))

    first, final = lane == 0, lane == nz - 1
    z_lo_mult = jnp.where(first, low_mult(2), 1.0) * scale
    z_hi_mult = high_mult(2) * scale
    def along_z(x, _):
        v = dz[x].astype(jnp.float32) * z_lo_mult
        g = gain(v)

        def ghosts(ref, f):
            back = lax.rem(nz - 4 * lax.rem(f * nx + x, per), nz)
            return pltpu.roll(ref[f * nx // per], back, 1)

        vh = ghosts(cq, 5) * z_hi_mult
        gh = gain(vh)
        for f in range(5):
            plane = q[f, x, SUB:top]
            gq, gs = ghosts(cq, f), ghosts(cs, f)
            qm = jnp.where(first, gq, pltpu.roll(plane, 1, 1))
            d = plane - qm
            s = minmod(jnp.where(final, gq - plane, pltpu.roll(d, nz - 1, 1)), d)
            sm = jnp.where(first, gs, pltpu.roll(s, 1, 1))
            fl = flux(v, g, qm, plane, sm, s)
            fh = jnp.where(final, flux(vh, gh, plane, gq, s, gs), pltpu.roll(fl, nz - 1, 1))
            outs[f](x)[...] += fl - fh
        return 0

    lax.fori_loop(0, nx, along_z, 0)

    @pl.when(relays)
    def _():
        for a, b in zip(legs_up, onward):
            a.wait_recv()
            b.start()

    def y_low():
        q[:, :, 0:SUB] = jnp.broadcast_to(q[:, :, SUB : SUB + 1], (5, nx, SUB, nz))

    def y_high():
        q[:, :, hi_rows] = jnp.broadcast_to(q[:, :, top - 1 : top], (5, nx, SUB, nz))
        dy[:, hi_rows] = jnp.broadcast_to(dy[:, top - 1 : top], (nx, SUB, nz))

    arrive("gy", y_up, y_down, y_low, y_high)
    tall = ny + 2 * SUB
    rows = lax.broadcasted_iota(jnp.int32, (tall, nz), 0)
    inside = (rows >= SUB) & (rows <= top)
    y_mult = jnp.where(
        rows == SUB, low_mult(1) * scale, jnp.where(rows == top, high_mult(1) * scale, scale)
    )

    def along_y(x, _):
        v = jnp.where(inside, dy[x].astype(jnp.float32), 0.0) * y_mult
        g = gain(v)
        for f in range(5):
            plane = q[f, x]
            qm = pltpu.roll(plane, 1, 0)
            d = plane - qm
            s = minmod(pltpu.roll(d, tall - 1, 0), d)
            fl = flux(v, g, qm, plane, pltpu.roll(s, 1, 0), s)
            ch = fl - pltpu.roll(fl, tall - 1, 0)
            outs[f](x)[...] += ch[SUB:top]
        return 0

    lax.fori_loop(0, nx, along_y, 0)

    def x_low():
        xlo[...] = jnp.broadcast_to(q[:, 0:1, SUB:top], (5, 2, ny, nz))

    def x_high():
        xhi[...] = jnp.broadcast_to(q[:, nx - 1 : nx, SUB:top], (5, 2, ny, nz))
        xv[...] = dx[nx - 1]

    arrive("gx", x_up, x_down, x_low, x_high)
    x_lo_mult, x_hi_mult = low_mult(0) * scale, high_mult(0) * scale

    def x_rows(r):
        return pl.ds(pl.multiple_of(r * SUB, SUB), SUB), pl.ds(
            pl.multiple_of(r * SUB + SUB, SUB), SUB
        )

    def x_flux(v, g, cells4):
        ds = [cells4[i + 1] - cells4[i] for i in range(3)]
        return flux(
            v, g, cells4[1], cells4[2], minmod(ds[1], ds[0]), minmod(ds[2], ds[1])
        )

    def rim(fields, r, _):
        at, inner = x_rows(r)
        faces = (0, 1, nx - 1, nx)
        vs = [
            dx[0, at].astype(jnp.float32) * x_lo_mult,
            dx[1, at].astype(jnp.float32) * scale,
            dx[nx - 1, at].astype(jnp.float32) * scale,
            xv[at].astype(jnp.float32) * x_hi_mult,
        ]
        gs = [gain(v) for v in vs]
        for f in fields:
            a = [xlo[f, 0, at], xlo[f, 1, at]] + [q[f, c, inner] for c in range(3)]
            b = [q[f, c, inner] for c in range(nx - 3, nx)] + [xhi[f, 0, at], xhi[f, 1, at]]
            fl = [x_flux(vs[i], gs[i], (a, a, b, b)[i][i % 2 : i % 2 + 4]) for i in range(4)]
            for c, change in (
                (0, fl[0] - fl[1]), (1, fl[1]), (nx - 2, -fl[2]), (nx - 1, fl[2] - fl[3]),
            ):
                ref = outs[f](c)
                ref[at] += change
        return 0

    lax.fori_loop(0, ny // SUB, functools.partial(rim, (0, 3)), 0)
    for piece, whole, fields in ((0, (0,), (1,)), (1, (), (2,)), (2, (1,), (4,))):
        each(low_half, [x_up_half[k] for k in whole], lambda c: c.wait_recv())
        each(high_half, [x_down_half[k] for k in whole], lambda c: c.wait_recv())
        each(leg_in, landed[piece : piece + 1], lambda c: c.wait_recv())
        lax.fori_loop(0, ny // SUB, functools.partial(rim, fields), 0)

    @pl.when(first_device)
    def _():
        gathered.wait_recv()
        done[...] = part[...] + jnp.sum(slots[1:count], 0)

        def tell(i, _):
            message(done, done, 1, place(i)).start()
            return 0

        lax.fori_loop(1, count, tell, 0)
        scattered.wait_send()

    @pl.when(~first_device)
    def _():
        outward.wait_recv()
        inward.wait_send()

    sums[...] = done[...]
    each(above_x, x_up, lambda c: c.wait_send())
    each(below_x, x_down, lambda c: c.wait_send())
    each(leg_out, legs_up, lambda c: c.wait_send())
    each(relays, onward, lambda c: c.wait_send())
    each(up_half, x_up_half, lambda c: c.wait_send())
    each(down_half, x_down_half, lambda c: c.wait_send())
    each(above_y, y_up, lambda c: c.wait_send())
    each(below_y, y_down, lambda c: c.wait_send())
    each(above_z, z_up, lambda c: c.wait_send())
    each(below_z, z_down, lambda c: c.wait_send())


def put(cells, den, mom, en, sums, out_d, out_m, out_e, totals, mean, sem):
    pairs = ((mom, out_m), (den, out_d), (en, out_e))
    moves = [
        pltpu.make_async_copy(src, dst, sem.at[i]) for i, (src, dst) in enumerate(pairs)
    ]
    for c in moves:
        c.start()
    mean[0] = jnp.sum(sums[0:1]) / cells
    mean[1] = jnp.sum(sums[1:2]) / cells
    moves.append(pltpu.make_async_copy(mean, totals, sem.at[3]))
    moves[-1].start()
    for c in moves:
        c.wait()


def shards(density, momentum, energy, displacement, flags):
    sizes = {a: lax.axis_size(a) for a in AXES}
    nx, ny, nz = density.shape
    tall = ny + 2 * SUB
    per = nz // 4
    parts = -(-6 * nx // per)
    f32, i32 = jnp.float32, jnp.int32
    dma = pltpu.SemaphoreType.DMA
    any_ = pl.BlockSpec(memory_space=pl.ANY)
    hbm = pl.BlockSpec(memory_space=pltpu.HBM)
    vmem = pl.BlockSpec(memory_space=pltpu.VMEM)
    devices = 1
    for a in AXES:
        devices *= sizes[a]
    cells = float(nx * ny * nz * devices)
    outputs = tuple(jax.ShapeDtypeStruct(v.shape, f32) for v in (density, momentum, energy))
    results = pl.pallas_call(
        functools.partial(kernel, sizes),
        out_shape=outputs + (jax.ShapeDtypeStruct((2, nz), f32),),
        in_specs=[hbm] * 5,
        out_specs=(vmem, vmem, vmem, vmem),
        scratch_shapes=[
            pltpu.SMEM((6,), i32),
            pltpu.VMEM((5, nx, tall, nz), f32),
            pltpu.VMEM((nx, ny, nz), i32),
            pltpu.VMEM((nx, tall, nz), i32),
            pltpu.VMEM((nx, ny, nz), i32),
            pltpu.VMEM((2, 5, 2, ny, nz), f32),
            pltpu.VMEM((5, ny, nz), f32),
            pltpu.VMEM((ny, nz), i32),
        ]
        + [pltpu.VMEM((parts, ny, nz), f32) for _ in range(5)]
        + [pltpu.VMEM((2, nz), f32), pltpu.VMEM((devices, 2, nz), f32), pltpu.VMEM((2, nz), f32)]
        + [dma((7,)), dma((26,)), dma((26,)), pltpu.SemaphoreType.REGULAR((4,)), dma((2,)), dma((2,))],
        compiler_params=pltpu.CompilerParams(
            collective_id=0, has_side_effects=True, vmem_limit_bytes=12 << 20
        ),
    )(
        *(
            pltpu.with_memory_space_constraint(v, pltpu.HBM)
            for v in (flags, density, momentum, energy, displacement)
        )
    )
    return pl.pallas_call(
        functools.partial(put, cells),
        out_shape=outputs + (jax.ShapeDtypeStruct((2,), f32),),
        in_specs=[any_, any_, any_, vmem],
        out_specs=(hbm, hbm, hbm, hbm),
        scratch_shapes=[pltpu.SMEM((2,), f32), dma((4,))],
        compiler_params=pltpu.CompilerParams(vmem_limit_bytes=2 << 20),
    )(*results)


def solution(mesh):
    return jax.shard_map(
        shards,
        mesh=mesh,
        in_specs=(
            P("gx", "gy", "gz"),
            P(None, "gx", "gy", "gz"),
            P("gx", "gy", "gz"),
            P(None, "gx", "gy", "gz"),
            P(),
        ),
        out_specs=(P("gx", "gy", "gz"), P(None, "gx", "gy", "gz"), P("gx", "gy", "gz"), P()),
        check_vma=False,
    )
```

time: 22.8 us -> 20.8 us (0.912)
  Pallas kernels: 22 us -> 20 us
    pallas_call x1, Pallas kernels: 20.4 us -> 18.9 us  [shards(): pl.pallas_call(functools.partial(kernel, sizes), out_shape=outputs + (jax...]
    pallas_call x1, Pallas kernels: 1.59 us -> 1.09 us  [shards(): pl.pallas_call(functools.partial(put, cells), out_shape=outputs + (jax.Sh...]
where the time goes in v1:
time: 20.8 us; the launch traced here: 20.7 us
  Pallas kernels  20 us (96%)
  between operations  0.64 us (3%)
    pallas_call x1, Pallas kernels, shards(): pl.pallas_call(functools.partial(kernel, sizes), out_shape=outputs + (jax...  18.9 us
    pallas_call x1, Pallas kernels, shards(): pl.pallas_call(functools.partial(put, cells), out_shape=outputs + (jax.Sh...  1.09 us

profile of v1, /device:TPU:0, one launch (start us, length us, event | category | flops | bytes accessed | tf_op | source)
XLA Modules:
  0.0 20.7 jit_solution(10794919983768012155)
XLA Ops:
  0.6 18.9 %shard_map.84 = (f32[8,64,128]{2,1,0:T(8,128)S(1)}, f32[3,8,64,128]{3,2,1,0:T(8,128)S(1)}, f32[8,64,128]{2,1,0:T(8,128)S(1)}, f32[2,128]{1,0:T(2,128)S(1)}) custom-call(s32[6]{0:T(128)} %flags_in.1, f32[8,64,128]{2,1,0:T(8,128)} %den.1, f32[3,8,64,128]{3,2,1,0:T(8,128)} %mom.1, f32[8,64,128]{2,1,0:T(8,128)} %en.1, s32[3,8,64,128]{3,2,1,0:T(8,128)} %disp.1), custom_call_target="tpu_custom_call" | custom-call | tf_op jit(solution)/shard_map/pallas_call | solution.py:519
  19.6 1.1 %shard_map.85 = (f32[8,64,128]{2,1,0:T(8,128)}, f32[3,8,64,128]{3,2,1,0:T(8,128)}, f32[8,64,128]{2,1,0:T(8,128)}, f32[2]{0:T(128)}) custom-call(f32[8,64,128]{2,1,0:T(8,128)S(1)} %get-tuple-element.8.den, f32[3,8,64,128]{3,2,1,0:T(8,128)S(1)} %get-tuple-element.9.mom, f32[8,64,128]{2,1,0:T(8,128)S(1)} %get-tuple-element.10.en, ...), custom_call_target="tpu_custom_call" | custom-call | tf_op jit(solution)/shard_map/pallas_call | solution.py:546

commit v2 on v1

--- a/solution.py
+++ b/solution.py
@@ -27,7 +27,7 @@
 
 def kernel(
     sizes, flags_in, den, mom, en, disp, out_d, out_m, out_e, sums,
-    flags, q, dx, dy, dz, xh, hop, xv, edge, zlo, zhi, cq, cs, part, slots, done,
+    flags, q, dx, dy, dz, xh, hop, xv, edge, zlo, zhi, cq, cs, part, slots, line, done,
     local_sem, send_sem, recv_sem, in_sem, sum_send, sum_recv,
 ):
     nx, ny, nz = den.shape
@@ -41,48 +41,70 @@
     own = slice(SUB, top)
     mesh_ids = pl.DeviceIdType.MESH
 
-    locals_ = [
-        pltpu.make_async_copy(flags_in, flags, local_sem.at[6]),
-        pltpu.make_async_copy(den, q.at[0, :, own], local_sem.at[0]),
-        pltpu.make_async_copy(en, q.at[4, :, own], local_sem.at[2]),
-        pltpu.make_async_copy(disp.at[2], dz, local_sem.at[3]),
-        pltpu.make_async_copy(disp.at[1], dy.at[:, own], local_sem.at[4]),
-        pltpu.make_async_copy(disp.at[0], dx, local_sem.at[5]),
-        pltpu.make_async_copy(mom, q.at[1:4, :, own], local_sem.at[1]),
+    def load(src, dst, k):
+        return pltpu.make_async_copy(src, dst, local_sem.at[k])
+
+    spans = (slice(0, 2), slice(nx - 2, nx), slice(2, nx - 2))
+    planes = [
+        [
+            load(den.at[x], q.at[0, x, own], 3 * i),
+            load(en.at[x], q.at[4, x, own], 3 * i + 1),
+            load(mom.at[:, x], q.at[1:4, x, own], 3 * i + 2),
+        ]
+        for i, x in enumerate(spans)
     ]
-    for c in locals_:
+    others = [
+        load(disp.at[0], dx, 9),
+        load(flags_in, flags, 10),
+        load(disp.at[2], dz, 11),
+        load(disp.at[1], dy.at[:, own], 12),
+    ]
+    for c in planes[0] + planes[1] + others + planes[2]:
         c.start()
 
     me = pos["gx"]
     par = lax.rem(me, 2)
     odd = par == 1
     end = last["gx"]
-    reach = [("gx", 1, 0, me > 0), ("gx", 2, 1, odd), ("gy", 1, 2, True), ("gz", 1, 3, True)]
+    sx, sy, sz = (sizes[a] for a in AXES)
+    group = sx * sz
+    leader = (me == 0) & (pos["gz"] == last["gz"])
+    members = [{"gx": i // sz, "gz": last["gz"] - i % sz} for i in range(1, group)]
+
+    def tell(sem, cond, **target):
+        @pl.when(cond)
+        def _():
+            pl.semaphore_signal(sem, inc=1, device_id=target, device_id_type=mesh_ids)
 
     barrier = pltpu.get_barrier_semaphore()
-    below = sum(jnp.where(pos[a] >= o, 1, 0) for a, o, _, _ in reach)
+    reach = [("gx", 1, par == 0, odd), ("gx", 2, True, True), ("gy", 1, True, True), ("gz", 1, True, True)]
+    below = jnp.where(leader, pos["gy"], 1)
+    for a, o, speaks, hears in reach:
+        tell(barrier, (pos[a] + o <= last[a]) & speaks, **{a: pos[a] + o})
+        below += jnp.where((pos[a] >= o) & hears, 1, 0)
+
+    @pl.when(leader)
+    def _():
+        for target in members:
+            tell(barrier, True, **target)
+        for o in range(1, sy):
+            tell(barrier, pos["gy"] + o <= last["gy"], gy=pos["gy"] + o)
 
     @pl.when(below > 0)
     def _():
         pl.semaphore_wait(barrier, below)
 
-    for a, o, k, told in reach:
-        @pl.when(pos[a] + o <= last[a])
-        def _(a=a, o=o):
-            pl.semaphore_signal(
-                barrier, inc=1, device_id={a: pos[a] + o}, device_id_type=mesh_ids
-            )
-
-        @pl.when((pos[a] >= o) & told)
-        def _(a=a, o=o, k=k):
-            pl.semaphore_signal(
-                in_sem.at[k], inc=1, device_id={a: pos[a] - o}, device_id_type=mesh_ids
-            )
-
-    def is_in(a, o, k, cond=True):
-        @pl.when((pos[a] + o <= last[a]) & cond)
-        def _():
-            pl.semaphore_wait(in_sem.at[k], 1)
+    tell(in_sem.at[0], odd, gx=me - 1)
+    tell(in_sem.at[1], me >= 2, gx=me - 2)
+    tell(in_sem.at[2], pos["gy"] > 0, gy=pos["gy"] - 1)
+    tell(in_sem.at[3], pos["gz"] > 0, gz=pos["gz"] - 1)
+    for o in range(1, sy):
+        tell(in_sem.at[4], leader & (pos["gy"] >= o), gy=pos["gy"] - o)
+
+    def is_in(k, cond, many=1):
+        @pl.when(cond)
+        def _():
+            pl.semaphore_wait(in_sem.at[k], many)
 
     def copy(k, src, dst, axis, step):
         return pltpu.make_async_remote_copy(
@@ -90,57 +112,37 @@
             device_id={axis: pos[axis] + step}, device_id_type=mesh_ids,
         )
 
-    leg_up = odd & (me + 2 <= end)
-    leg_down = (par == 0) & (me >= 2)
-    leg_out = leg_up | leg_down
-    relays = (odd & (me >= 3)) | ((par == 0) & (me + 2 <= end))
-    leg_in = (me + 1 <= end) & (odd | (me >= 2))
-    other = 1 - par
-
+    below_x, below_y, below_z = me > 0, pos["gy"] > 0, pos["gz"] > 0
+    above_x, above_y, above_z = (pos[a] < last[a] for a in AXES)
+    even = ~odd
+    hands_up, hands_down = odd & above_x, even & below_x
+    relays = (odd & below_x & (me >= 3)) | (even & (me + 2 <= end))
+    beside = 1 - 2 * par
+
+    order = (0, 3, 1, 2, 4)
+    direct = (0, 3)
+    relayed = (1, 2)
+    up = {f: copy(f, q.at[f, nx - 2 : nx, own], xlo.at[f], "gx", 1) for f in order}
+    down = {f: copy(5 + f, q.at[f, 0:2, own], xhi.at[f], "gx", -1) for f in order}
+    down_last = copy(9, q.at[4, 1, own], xhi.at[4, 1], "gx", -1)
+    up_last = copy(4, q.at[4, nx - 1, own], xlo.at[4, 1], "gx", 1)
+    v_down = copy(10, dx.at[0], xv, "gx", -1)
     legs_up = [
-        copy(16, q.at[1, nx - 2 : nx, own], hop.at[0:2], "gx", 2),
-        copy(17, q.at[2, nx - 2 : nx, own], hop.at[2:4], "gx", 2),
-        copy(18, q.at[4, nx - 2, own], hop.at[4], "gx", 2),
-    ]
+        copy(16 + i, q.at[f, nx - 2 : nx, own], hop.at[2 * i : 2 * i + 2], "gx", 2)
+        for i, f in enumerate(relayed)
+    ] + [copy(18, q.at[4, nx - 2, own], hop.at[4], "gx", 2)]
     legs_down = [
-        copy(16, mom.at[0, 0:2], hop.at[0:2], "gx", -2),
-        copy(17, mom.at[1, 0:2], hop.at[2:4], "gx", -2),
-        copy(18, en.at[0], hop.at[4], "gx", -2),
-    ]
-    beside = 1 - 2 * par
-    onward = [
-        copy(19, hop.at[0:2], xh.at[other, 1], "gx", beside),
-        copy(20, hop.at[2:4], xh.at[other, 2], "gx", beside),
-        copy(21, hop.at[4], xh.at[other, 4, 0], "gx", beside),
-    ]
-    landed = [
-        copy(19, hop.at[0:2], xh.at[par, 1], "gx", beside),
-        copy(20, hop.at[2:4], xh.at[par, 2], "gx", beside),
-        copy(21, hop.at[4], xh.at[par, 4, 0], "gx", beside),
-    ]
-    x_up = [
-        copy(0, q.at[0, nx - 2 : nx, own], xlo.at[0], "gx", 1),
-        copy(1, q.at[3, nx - 2 : nx, own], xlo.at[3], "gx", 1),
-        copy(2, q.at[4, nx - 1, own], xlo.at[4, 1], "gx", 1),
-    ]
-    x_up_half = [
-        copy(22, q.at[1:3, nx - 2 : nx, own], xlo.at[1:3], "gx", 1),
-        copy(23, q.at[4, nx - 2, own], xlo.at[4, 0], "gx", 1),
-    ]
-    x_down = [
-        copy(6, disp.at[0, 0], xv, "gx", -1),
-        copy(3, den.at[0:2], xhi.at[0], "gx", -1),
-        copy(4, mom.at[2, 0:2], xhi.at[3], "gx", -1),
-        copy(5, en.at[1], xhi.at[4, 1], "gx", -1),
-    ]
-    x_down_half = [
-        copy(24, mom.at[0:2, 0:2], xhi.at[1:3], "gx", -1),
-        copy(25, en.at[0], xhi.at[4, 0], "gx", -1),
-    ]
-    up_half = (me < end) & ~leg_up
-    down_half = (me > 0) & ~leg_down
-    low_half = (me > 0) & ~(leg_in & (par == 0))
-    high_half = (me < end) & ~(leg_in & odd)
+        copy(16 + i, q.at[f, 0:2, own], hop.at[2 * i : 2 * i + 2], "gx", -2)
+        for i, f in enumerate(relayed)
+    ] + [copy(18, q.at[4, 0, own], hop.at[4], "gx", -2)]
+
+    def handed(side):
+        return [
+            copy(19 + i, hop.at[2 * i : 2 * i + 2], side.at[f], "gx", beside)
+            for i, f in enumerate(relayed)
+        ] + [copy(21, hop.at[4], side.at[4, 0], "gx", beside)]
+
+    handed_up, handed_down = handed(xlo), handed(xhi)
 
     def each(cond, copies, act):
         @pl.when(cond)
@@ -153,15 +155,15 @@
 
     hi_rows = slice(top, top + SUB)
     y_up = [
-        copy(7, q.at[0, :, ny:top], q.at[0, :, 0:SUB], "gy", 1),
-        copy(8, q.at[1:4, :, ny:top], q.at[1:4, :, 0:SUB], "gy", 1),
-        copy(9, q.at[4, :, ny:top], q.at[4, :, 0:SUB], "gy", 1),
+        copy(22, q.at[0, :, ny:top], q.at[0, :, 0:SUB], "gy", 1),
+        copy(23, q.at[1:4, :, ny:top], q.at[1:4, :, 0:SUB], "gy", 1),
+        copy(24, q.at[4, :, ny:top], q.at[4, :, 0:SUB], "gy", 1),
     ]
     y_down = [
-        copy(10, den.at[:, 0:SUB], q.at[0, :, hi_rows], "gy", -1),
-        copy(11, mom.at[:, :, 0:SUB], q.at[1:4, :, hi_rows], "gy", -1),
-        copy(12, en.at[:, 0:SUB], q.at[4, :, hi_rows], "gy", -1),
-        copy(13, disp.at[1, :, 0:SUB], dy.at[:, hi_rows], "gy", -1),
+        copy(11, q.at[4, :, SUB : 2 * SUB], q.at[4, :, hi_rows], "gy", -1),
+        copy(12, q.at[0, :, SUB : 2 * SUB], q.at[0, :, hi_rows], "gy", -1),
+        copy(13, q.at[1:4, :, SUB : 2 * SUB], q.at[1:4, :, hi_rows], "gy", -1),
+        copy(25, dy.at[:, SUB : 2 * SUB], dy.at[:, hi_rows], "gy", -1),
     ]
     z_up = [copy(14, edge, zlo, "gz", 1)]
     z_down = [copy(15, edge, zhi, "gz", -1)]
@@ -196,14 +198,10 @@
             for c in downs:
                 c.wait_send()
 
-    below_x, below_y, below_z = me > 0, pos["gy"] > 0, pos["gz"] > 0
-    above_x, above_y, above_z = (pos[a] < last[a] for a in AXES)
-    each(leg_down, legs_down, go)
-    each(below_x, x_down, go)
-    each(down_half, x_down_half, go)
-    each(below_y, y_down, go)
-
-    for c in locals_[:-1]:
+    first, rest = order[0], order[1:]
+    planes[0][0].wait()
+    each(odd, [down[first]], go)
+    for c in planes[0][1:] + planes[1] + others + planes[2]:
         c.wait()
 
     flag = [flags[i].astype(jnp.float32) for i in range(6)]
@@ -244,31 +242,46 @@
     part[0:1] = jnp.sum(mass, 0, keepdims=True)
     part[1:2] = jnp.sum(power, 0, keepdims=True)
 
-    sx, sy, sz = (sizes[a] for a in AXES)
-    count = sx * sy * sz
-    index = (pos["gx"] * sy + pos["gy"]) * sz + pos["gz"]
-    first_device = index == 0
-
-    def place(i):
-        return {"gx": i // (sy * sz), "gy": i // sz % sy, "gz": i % sz}
-
     def message(src, dst, k, target):
         return pltpu.make_async_remote_copy(
             src_ref=src, dst_ref=dst, send_sem=sum_send.at[k], recv_sem=sum_recv.at[k],
             device_id=target, device_id_type=mesh_ids,
         )
 
-    away = place(count - 1)
-    inward = message(part, slots.at[index], 0, place(0))
-    gathered = message(slots.at[1:count], slots.at[1:count], 0, away)
-    outward = message(done, done, 1, place(0))
-    scattered = message(slots.at[1:count], slots.at[1:count], 1, away)
-
-    @pl.when(~first_device)
-    def _():
-        inward.start()
-
-    locals_[-1].wait()
+    inward = message(part, slots.at[me * sz + last["gz"] - pos["gz"]], 0, {"gx": 0, "gz": last["gz"]})
+    gathered = message(slots.at[1:group], slots.at[1:group], 0, members[-1])
+    across = [
+        message(line.at[0], line.at[sy - o], 1, {"gy": lax.rem(pos["gy"] + o, sy)})
+        for o in range(1, sy)
+    ]
+    crossed = message(line.at[1:sy], line.at[1:sy], 1, {"gy": lax.rem(pos["gy"] + 1, sy)})
+    outward = [message(done, done, 2, target) for target in members]
+    scattered = message(slots.at[1:group], slots.at[1:group], 2, members[-1])
+
+    each(~leader, [inward], go)
+
+    each(hands_down, legs_down, go)
+    each(below_y, y_down, go)
+
+    def x_sends():
+        is_in(0, even & above_x)
+        each(even & below_x & above_x, [up[f] for f in direct], go)
+        is_in(1, me + 2 <= end)
+
+        @pl.when(even & (me + 2 <= end))
+        def _():
+            tell(in_sem.at[5], True, gx=me + 1)
+            tell(in_sem.at[5], True, gx=me + 2)
+
+        each(odd, [v_down] + [down[f] for f in rest], go)
+        each(odd & (me + 2 <= end), legs_up, go)
+        each(~below_x & above_x, [up[f] for f in direct], go)
+        is_in(5, hands_up | hands_down)
+        each(hands_up, [up[f] for f in direct] + [up_last], go)
+        each(hands_down, [v_down] + [down[f] for f in direct] + [down_last], go)
+        each(even & above_x, [up[f] for f in relayed + (4,)], go)
+
+    pl.when(below_x | below_y)(x_sends)
 
     def pack(x, carry):
         new = list(carry)
@@ -286,14 +299,10 @@
     for k in range(parts):
         edge[k] = packed[k]
     each(below_z, z_down, go)
-    is_in("gz", 1, 3)
+    is_in(3, above_z)
     each(above_z, z_up, go)
-    is_in("gx", 1, 0, me + 1 > 0)
-    each(above_x, x_up, go)
-    each(up_half, x_up_half, go)
-    is_in("gx", 2, 1, odd)
-    each(leg_up, legs_up, go)
-    is_in("gy", 1, 2)
+    pl.when(~below_x & ~below_y)(x_sends)
+    is_in(2, above_y)
     each(above_y, y_up, go)
 
     outs = (
@@ -368,13 +377,28 @@
             outs[f](x)[...] += fl - fh
         return 0
 
-    lax.fori_loop(0, nx, along_z, 0)
-
-    @pl.when(relays)
-    def _():
-        for a, b in zip(legs_up, onward):
-            a.wait_recv()
-            b.start()
+    early = nx * 5 // 8
+    lax.fori_loop(0, early, along_z, 0)
+
+    def gather():
+        gathered.wait_recv()
+        line[0] = part[...] + jnp.sum(slots[1:group], 0)
+        is_in(4, pos["gy"] < last["gy"], last["gy"] - pos["gy"])
+        for c in across:
+            c.start()
+
+    pl.when(leader & below_y)(gather)
+    lax.fori_loop(early, nx, along_z, 0)
+
+    def hand_on(cond, legs, onward):
+        @pl.when(relays & cond)
+        def _():
+            for a, b in zip(legs, onward):
+                a.wait_recv()
+                b.start()
+
+    hand_on(odd, legs_up, handed_up)
+    hand_on(even, legs_down, handed_down)
 
     def y_low():
         q[:, :, 0:SUB] = jnp.broadcast_to(q[:, :, SUB : SUB + 1], (5, nx, SUB, nz))
@@ -384,6 +408,7 @@
         dy[:, hi_rows] = jnp.broadcast_to(dy[:, top - 1 : top], (nx, SUB, nz))
 
     arrive("gy", y_up, y_down, y_low, y_high)
+    pl.when(leader & ~below_y)(gather)
     tall = ny + 2 * SUB
     rows = lax.broadcasted_iota(jnp.int32, (tall, nz), 0)
     inside = (rows >= SUB) & (rows <= top)
@@ -406,83 +431,136 @@
 
     lax.fori_loop(0, nx, along_y, 0)
 
-    def x_low():
-        xlo[...] = jnp.broadcast_to(q[:, 0:1, SUB:top], (5, 2, ny, nz))
-
-    def x_high():
-        xhi[...] = jnp.broadcast_to(q[:, nx - 1 : nx, SUB:top], (5, 2, ny, nz))
+    @pl.when(me == 0)
+    def _():
+        xlo[...] = jnp.broadcast_to(q[:, 0:1, own], (5, 2, ny, nz))
+
+    @pl.when(me == end)
+    def _():
+        xhi[...] = jnp.broadcast_to(q[:, nx - 1 : nx, own], (5, 2, ny, nz))
         xv[...] = dx[nx - 1]
 
-    arrive("gx", x_up, x_down, x_low, x_high)
+    each(above_x, [v_down], lambda c: c.wait_recv())
     x_lo_mult, x_hi_mult = low_mult(0) * scale, high_mult(0) * scale
 
-    def x_rows(r):
-        return pl.ds(pl.multiple_of(r * SUB, SUB), SUB), pl.ds(
-            pl.multiple_of(r * SUB + SUB, SUB), SUB
-        )
-
-    def x_flux(v, g, cells4):
-        ds = [cells4[i + 1] - cells4[i] for i in range(3)]
-        return flux(
-            v, g, cells4[1], cells4[2], minmod(ds[1], ds[0]), minmod(ds[2], ds[1])
-        )
-
-    def rim(fields, r, _):
-        at, inner = x_rows(r)
-        faces = (0, 1, nx - 1, nx)
-        vs = [
-            dx[0, at].astype(jnp.float32) * x_lo_mult,
-            dx[1, at].astype(jnp.float32) * scale,
-            dx[nx - 1, at].astype(jnp.float32) * scale,
-            xv[at].astype(jnp.float32) * x_hi_mult,
-        ]
-        gs = [gain(v) for v in vs]
-        for f in fields:
-            a = [xlo[f, 0, at], xlo[f, 1, at]] + [q[f, c, inner] for c in range(3)]
-            b = [q[f, c, inner] for c in range(nx - 3, nx)] + [xhi[f, 0, at], xhi[f, 1, at]]
-            fl = [x_flux(vs[i], gs[i], (a, a, b, b)[i][i % 2 : i % 2 + 4]) for i in range(4)]
-            for c, change in (
-                (0, fl[0] - fl[1]), (1, fl[1]), (nx - 2, -fl[2]), (nx - 1, fl[2] - fl[3]),
-            ):
+    def rim(high, f):
+        def rows(r, _):
+            at = pl.ds(pl.multiple_of(r * SUB, SUB), SUB)
+            inner = pl.ds(pl.multiple_of(r * SUB + SUB, SUB), SUB)
+            if high:
+                cells = [q[f, c, inner] for c in range(nx - 3, nx)] + [xhi[f, i, at] for i in range(2)]
+                vs = (dx[nx - 1, at].astype(jnp.float32) * scale, xv[at].astype(jnp.float32) * x_hi_mult)
+            else:
+                cells = [xlo[f, i, at] for i in range(2)] + [q[f, c, inner] for c in range(3)]
+                vs = (dx[0, at].astype(jnp.float32) * x_lo_mult, dx[1, at].astype(jnp.float32) * scale)
+            ds = [cells[i + 1] - cells[i] for i in range(4)]
+            ss = [minmod(ds[i + 1], ds[i]) for i in range(3)]
+            fl = [
+                flux(vs[i], gain(vs[i]), cells[i + 1], cells[i + 2], ss[i], ss[i + 1])
+                for i in range(2)
+            ]
+            if high:
+                changes = ((nx - 2, -fl[0]), (nx - 1, fl[0] - fl[1]))
+            else:
+                changes = ((0, fl[0] - fl[1]), (1, fl[1]))
+            for c, change in changes:
                 ref = outs[f](c)
                 ref[at] += change
-        return 0
-
-    lax.fori_loop(0, ny // SUB, functools.partial(rim, (0, 3)), 0)
-    for piece, whole, fields in ((0, (0,), (1,)), (1, (), (2,)), (2, (1,), (4,))):
-        each(low_half, [x_up_half[k] for k in whole], lambda c: c.wait_recv())
-        each(high_half, [x_down_half[k] for k in whole], lambda c: c.wait_recv())
-        each(leg_in, landed[piece : piece + 1], lambda c: c.wait_recv())
-        lax.fori_loop(0, ny // SUB, functools.partial(rim, fields), 0)
-
-    @pl.when(first_device)
-    def _():
-        gathered.wait_recv()
-        done[...] = part[...] + jnp.sum(slots[1:count], 0)
-
-        def tell(i, _):
-            message(done, done, 1, place(i)).start()
             return 0
 
-        lax.fori_loop(1, count, tell, 0)
+        lax.fori_loop(0, ny // SUB, rows, 0)
+
+    def come(cond, copies):
+        each(cond, copies, lambda c: c.wait_recv())
+
+    def lower(f):
+        come(odd, [up[f]])
+        if f in direct:
+            come(hands_down, [up[f]])
+        elif f in relayed:
+            come(hands_down, [handed_up[f - 1]])
+        else:
+            come(hands_down, [up_last, handed_up[2]])
+        rim(False, f)
+
+    def upper(f):
+        come(even & above_x, [down[f]])
+        if f in direct:
+            come(hands_up, [down[f]])
+        elif f in relayed:
+            come(hands_up, [handed_down[f - 1]])
+        else:
+            come(hands_up, [down_last, handed_down[2]])
+        rim(True, f)
+
+    def finish():
+        crossed.wait_recv()
+        done[...] = jnp.sum(line[...], 0)
+        for c in outward:
+            c.start()
+
+    @pl.when(hands_up)
+    def _():
+        for f in direct:
+            upper(f)
+        for f in order:
+            lower(f)
+        for f in relayed + (4,):
+            upper(f)
+
+    @pl.when(odd & ~above_x)
+    def _():
+        for f in order:
+            upper(f)
+        for f in order:
+            lower(f)
+
+    @pl.when(hands_down)
+    def _():
+        for f in order:
+            upper(f)
+        for f in order:
+            lower(f)
+
+    @pl.when(~below_x)
+    def _():
+        for f in order:
+            lower(f)
+        for f in direct:
+            upper(f)
+        pl.when(leader)(finish)
+        for f in relayed + (4,):
+            upper(f)
+
+    @pl.when(~leader)
+    def _():
+        outward[0].wait_recv()
+        inward.wait_send()
+
+    sums[...] = done[...]
+
+    @pl.when(leader)
+    def _():
+        crossed.wait_send()
         scattered.wait_send()
 
-    @pl.when(~first_device)
-    def _():
-        outward.wait_recv()
-        inward.wait_send()
-
-    sums[...] = done[...]
-    each(above_x, x_up, lambda c: c.wait_send())
-    each(below_x, x_down, lambda c: c.wait_send())
-    each(leg_out, legs_up, lambda c: c.wait_send())
-    each(relays, onward, lambda c: c.wait_send())
-    each(up_half, x_up_half, lambda c: c.wait_send())
-    each(down_half, x_down_half, lambda c: c.wait_send())
-    each(above_y, y_up, lambda c: c.wait_send())
-    each(below_y, y_down, lambda c: c.wait_send())
-    each(above_z, z_up, lambda c: c.wait_send())
-    each(below_z, z_down, lambda c: c.wait_send())
+    def sent(cond, copies):
+        each(cond, copies, lambda c: c.wait_send())
+
+    sent(below_x, [v_down] + [down[f] for f in direct])
+    sent(odd, [down[f] for f in relayed + (4,)])
+    sent(above_x, [up[f] for f in direct])
+    sent(even & above_x, [up[f] for f in relayed + (4,)])
+    sent(hands_up, [up_last])
+    sent(hands_down, [down_last])
+    sent(odd & (me + 2 <= end), legs_up)
+    sent(hands_down, legs_down)
+    sent(relays & odd, handed_up)
+    sent(relays & even, handed_down)
+    sent(above_y, y_up)
+    sent(below_y, y_down)
+    sent(above_z, z_up)
+    sent(below_z, z_down)
 
 
 def put(cells, den, mom, en, sums, out_d, out_m, out_e, totals, mean, sem):
@@ -532,8 +610,9 @@
             pltpu.VMEM((ny, nz), i32),
         ]
         + [pltpu.VMEM((parts, ny, nz), f32) for _ in range(5)]
-        + [pltpu.VMEM((2, nz), f32), pltpu.VMEM((devices, 2, nz), f32), pltpu.VMEM((2, nz), f32)]
-        + [dma((7,)), dma((26,)), dma((26,)), pltpu.SemaphoreType.REGULAR((4,)), dma((2,)), dma((2,))],
+        + [pltpu.VMEM((2, nz), f32), pltpu.VMEM((sizes["gx"] * sizes["gz"], 2, nz), f32)]
+        + [pltpu.VMEM((sizes["gy"], 2, nz), f32), pltpu.VMEM((2, nz), f32)]
+        + [dma((13,)), dma((26,)), dma((26,)), pltpu.SemaphoreType.REGULAR((6,)), dma((3,)), dma((3,))],
         compiler_params=pltpu.CompilerParams(
             collective_id=0, has_side_effects=True, vmem_limit_bytes=12 << 20
         ),

time: 20.8 us -> 17.4 us (0.84)
  the two profiles are of different devices: /device:TPU:0 before, /device:TPU:5 now
where the time goes in v2:
time: 17.4 us; the launch traced here: 17.2 us
  Pallas kernels  16.6 us (95%)
  between operations  0.64 us (4%)
    pallas_call x1, Pallas kernels, shards(): pl.pallas_call(functools.partial(kernel, sizes), out_shape=outputs + (jax...  15.5 us
    pallas_call x1, Pallas kernels, shards(): pl.pallas_call(functools.partial(put, cells), out_shape=outputs + (jax.Sh...  1.09 us

profile of v2, /device:TPU:5, one launch (start us, length us, event | category | flops | bytes accessed | tf_op | source)
XLA Modules:
  0.0 17.2 jit_solution(16876695292012620637)
XLA Ops:
  0.6 15.5 %shard_map.84 = (f32[8,64,128]{2,1,0:T(8,128)S(1)}, f32[3,8,64,128]{3,2,1,0:T(8,128)S(1)}, f32[8,64,128]{2,1,0:T(8,128)S(1)}, f32[2,128]{1,0:T(2,128)S(1)}) custom-call(s32[6]{0:T(128)} %flags_in.1, f32[8,64,128]{2,1,0:T(8,128)} %den.1, f32[3,8,64,128]{3,2,1,0:T(8,128)} %mom.1, f32[8,64,128]{2,1,0:T(8,128)} %en.1, s32[3,8,64,128]{3,2,1,0:T(8,128)} %disp.1), custom_call_target="tpu_custom_call" | custom-call | tf_op jit(solution)/shard_map/pallas_call | solution.py:597
  16.2 1.1 %shard_map.85 = (f32[8,64,128]{2,1,0:T(8,128)}, f32[3,8,64,128]{3,2,1,0:T(8,128)}, f32[8,64,128]{2,1,0:T(8,128)}, f32[2]{0:T(128)}) custom-call(f32[8,64,128]{2,1,0:T(8,128)S(1)} %get-tuple-element.8.den, f32[3,8,64,128]{3,2,1,0:T(8,128)S(1)} %get-tuple-element.9.mom, f32[8,64,128]{2,1,0:T(8,128)S(1)} %get-tuple-element.10.en, ...), custom_call_target="tpu_custom_call" | custom-call | tf_op jit(solution)/shard_map/pallas_call | solution.py:625

commit v3 on v2

--- a/solution.py
+++ b/solution.py
@@ -27,7 +27,7 @@
 
 def kernel(
     sizes, flags_in, den, mom, en, disp, out_d, out_m, out_e, sums,
-    flags, q, dx, dy, dz, xh, hop, xv, edge, zlo, zhi, cq, cs, part, slots, line, done,
+    flags, q, dxz, dy, xh, hop, xv, edge, zlo, zhi, cq, cs, part, slots, line, done,
     local_sem, send_sem, recv_sem, in_sem, sum_send, sum_recv,
 ):
     nx, ny, nz = den.shape
@@ -38,6 +38,7 @@
     parts = edge.shape[0]
     scale = 1.0 / 256.0
     xlo, xhi = xh.at[0], xh.at[1]
+    dx, dz = dxz.at[0], dxz.at[1]
     own = slice(SUB, top)
     mesh_ids = pl.DeviceIdType.MESH
 
@@ -45,22 +46,24 @@
         return pltpu.make_async_copy(src, dst, local_sem.at[k])
 
     spans = (slice(0, 2), slice(nx - 2, nx), slice(2, nx - 2))
-    planes = [
-        [
-            load(den.at[x], q.at[0, x, own], 3 * i),
-            load(en.at[x], q.at[4, x, own], 3 * i + 1),
-            load(mom.at[:, x], q.at[1:4, x, own], 3 * i + 2),
+    loads = []
+    for i, x in enumerate(spans):
+        loads += [
+            load(den.at[x], q.at[0, x, own], i),
+            load(en.at[x], q.at[4, x, own], max(i, 3 - 3 * i)),
+            load(mom.at[:, x], q.at[1:4, x, own], max(i, 3 - 3 * i)),
         ]
-        for i, x in enumerate(spans)
+    loads += [
+        load(flags_in, flags, 4),
+        load(disp.at[0], dx, 5),
+        load(disp.at[2], dz, 5),
+        load(disp.at[1], dy.at[:, own], 6),
     ]
-    others = [
-        load(disp.at[0], dx, 9),
-        load(flags_in, flags, 10),
-        load(disp.at[2], dz, 11),
-        load(disp.at[1], dy.at[:, own], 12),
-    ]
-    for c in planes[0] + planes[1] + others + planes[2]:
+    for c in loads:
         c.start()
+
+    def loaded(ref, k):
+        load(ref, ref, k).wait()
 
     me = pos["gx"]
     par = lax.rem(me, 2)
@@ -76,12 +79,23 @@
         def _():
             pl.semaphore_signal(sem, inc=1, device_id=target, device_id_type=mesh_ids)
 
+    even = ~odd
+    above = {a: pos[a] < last[a] for a in AXES}
+    above_x, above_y, above_z = (above[a] for a in AXES)
+    below_x, below_y, below_z = me > 0, pos["gy"] > 0, pos["gz"] > 0
+    over = me + 2 <= end
+    inner = even & below_x
     barrier = pltpu.get_barrier_semaphore()
-    reach = [("gx", 1, par == 0, odd), ("gx", 2, True, True), ("gy", 1, True, True), ("gz", 1, True, True)]
-    below = jnp.where(leader, pos["gy"], 1)
-    for a, o, speaks, hears in reach:
-        tell(barrier, (pos[a] + o <= last[a]) & speaks, **{a: pos[a] + o})
-        below += jnp.where((pos[a] >= o) & hears, 1, 0)
+    greetings = [
+        (even & above_x, odd, {"gx": me + 1}),
+        (over, me >= 2, {"gx": me + 2}),
+        (above_y, below_y, {"gy": pos["gy"] + 1}),
+        (above_z, below_z, {"gz": pos["gz"] + 1}),
+    ]
+    heard = jnp.where(leader, pos["gy"], 1)
+    for speaks, hears, target in greetings:
+        tell(barrier, speaks, **target)
+        heard += jnp.where(hears, 1, 0)
 
     @pl.when(leader)
     def _():
@@ -90,57 +104,62 @@
         for o in range(1, sy):
             tell(barrier, pos["gy"] + o <= last["gy"], gy=pos["gy"] + o)
 
-    @pl.when(below > 0)
-    def _():
-        pl.semaphore_wait(barrier, below)
+    @pl.when(heard > 0)
+    def _():
+        pl.semaphore_wait(barrier, heard)
 
     tell(in_sem.at[0], odd, gx=me - 1)
-    tell(in_sem.at[1], me >= 2, gx=me - 2)
-    tell(in_sem.at[2], pos["gy"] > 0, gy=pos["gy"] - 1)
-    tell(in_sem.at[3], pos["gz"] > 0, gz=pos["gz"] - 1)
+    tell(in_sem.at[0], me >= 2, gx=me - 2)
+    tell(in_sem.at[2], below_y, gy=pos["gy"] - 1)
+    tell(in_sem.at[2], below_z, gz=pos["gz"] - 1)
     for o in range(1, sy):
-        tell(in_sem.at[4], leader & (pos["gy"] >= o), gy=pos["gy"] - o)
+        tell(in_sem.at[3], leader & (pos["gy"] >= o), gy=pos["gy"] - o)
 
     def is_in(k, cond, many=1):
         @pl.when(cond)
         def _():
             pl.semaphore_wait(in_sem.at[k], many)
 
-    def copy(k, src, dst, axis, step):
+    def copy(ks, kr, src, dst, axis, step):
         return pltpu.make_async_remote_copy(
-            src_ref=src, dst_ref=dst, send_sem=send_sem.at[k], recv_sem=recv_sem.at[k],
+            src_ref=src, dst_ref=dst, send_sem=send_sem.at[ks], recv_sem=recv_sem.at[kr],
             device_id={axis: pos[axis] + step}, device_id_type=mesh_ids,
         )
 
-    below_x, below_y, below_z = me > 0, pos["gy"] > 0, pos["gz"] > 0
-    above_x, above_y, above_z = (pos[a] < last[a] for a in AXES)
-    even = ~odd
-    hands_up, hands_down = odd & above_x, even & below_x
-    relays = (odd & below_x & (me >= 3)) | (even & (me + 2 <= end))
+    hands_up, hands_down = odd & above_x, inner
+    relays = (odd & (me >= 3)) | (even & over)
     beside = 1 - 2 * par
-
-    order = (0, 3, 1, 2, 4)
-    direct = (0, 3)
-    relayed = (1, 2)
-    up = {f: copy(f, q.at[f, nx - 2 : nx, own], xlo.at[f], "gx", 1) for f in order}
-    down = {f: copy(5 + f, q.at[f, 0:2, own], xhi.at[f], "gx", -1) for f in order}
-    down_last = copy(9, q.at[4, 1, own], xhi.at[4, 1], "gx", -1)
-    up_last = copy(4, q.at[4, nx - 1, own], xlo.at[4, 1], "gx", 1)
-    v_down = copy(10, dx.at[0], xv, "gx", -1)
+    main, across_x, legs_k, hand_k = 0, 1, 3, 4
+
+    groups = (slice(3, 5), slice(1, 3), 0)
+    tops, bottoms = slice(nx - 2, nx), slice(0, 2)
+
+    def piece(k, i, x, side, first, step):
+        f = groups[i]
+        return copy(k, first + i, q.at[f, x, own], side.at[f], "gx", step)
+
+    def one(k, r, x, side, i, step):
+        return copy(k, r, q.at[0, x, own], side.at[0, i], "gx", step)
+
+    up = [piece(main, i, tops, xlo, 0, 1) for i in range(3)]
+    down = [piece(main, i, bottoms, xhi, 3, -1) for i in range(3)]
+    v_down = copy(2, 6, dx.at[0], xv, "gx", -1)
+    up_across = [piece(across_x, 0, tops, xlo, 0, 1), one(across_x, 2, nx - 1, xlo, 1, 1)]
+    down_across = [piece(across_x, 0, bottoms, xhi, 3, -1), one(across_x, 5, 1, xhi, 1, -1)]
     legs_up = [
-        copy(16 + i, q.at[f, nx - 2 : nx, own], hop.at[2 * i : 2 * i + 2], "gx", 2)
-        for i, f in enumerate(relayed)
-    ] + [copy(18, q.at[4, nx - 2, own], hop.at[4], "gx", 2)]
+        copy(legs_k, 7, q.at[1:3, tops, own], hop.at[0:2], "gx", 2),
+        copy(legs_k, 8, q.at[0, nx - 2, own], hop.at[2, 0], "gx", 2),
+    ]
     legs_down = [
-        copy(16 + i, q.at[f, 0:2, own], hop.at[2 * i : 2 * i + 2], "gx", -2)
-        for i, f in enumerate(relayed)
-    ] + [copy(18, q.at[4, 0, own], hop.at[4], "gx", -2)]
+        copy(legs_k, 7, q.at[1:3, bottoms, own], hop.at[0:2], "gx", -2),
+        copy(legs_k, 8, q.at[0, 0, own], hop.at[2, 0], "gx", -2),
+    ]
 
     def handed(side):
         return [
-            copy(19 + i, hop.at[2 * i : 2 * i + 2], side.at[f], "gx", beside)
-            for i, f in enumerate(relayed)
-        ] + [copy(21, hop.at[4], side.at[4, 0], "gx", beside)]
+            copy(hand_k, 9, hop.at[0:2], side.at[1:3], "gx", beside),
+            copy(hand_k, 10, hop.at[2, 0], side.at[0, 0], "gx", beside),
+        ]
 
     handed_up, handed_down = handed(xlo), handed(xhi)
 
@@ -154,19 +173,13 @@
         c.start()
 
     hi_rows = slice(top, top + SUB)
-    y_up = [
-        copy(22, q.at[0, :, ny:top], q.at[0, :, 0:SUB], "gy", 1),
-        copy(23, q.at[1:4, :, ny:top], q.at[1:4, :, 0:SUB], "gy", 1),
-        copy(24, q.at[4, :, ny:top], q.at[4, :, 0:SUB], "gy", 1),
+    y_up = [copy(5, 11, q.at[:, :, ny:top], q.at[:, :, 0:SUB], "gy", 1)]
+    y_down = [
+        copy(6, 12, q.at[:, :, SUB : 2 * SUB], q.at[:, :, hi_rows], "gy", -1),
+        copy(7, 13, dy.at[:, SUB : 2 * SUB], dy.at[:, hi_rows], "gy", -1),
     ]
-    y_down = [
-        copy(11, q.at[4, :, SUB : 2 * SUB], q.at[4, :, hi_rows], "gy", -1),
-        copy(12, q.at[0, :, SUB : 2 * SUB], q.at[0, :, hi_rows], "gy", -1),
-        copy(13, q.at[1:4, :, SUB : 2 * SUB], q.at[1:4, :, hi_rows], "gy", -1),
-        copy(25, dy.at[:, SUB : 2 * SUB], dy.at[:, hi_rows], "gy", -1),
-    ]
-    z_up = [copy(14, edge, zlo, "gz", 1)]
-    z_down = [copy(15, edge, zhi, "gz", -1)]
+    z_up = [copy(8, 14, edge, zlo, "gz", 1)]
+    z_down = [copy(9, 15, edge, zhi, "gz", -1)]
 
     def arrive(axis, ups, downs, fill_low, fill_high):
         @pl.when(pos[axis] > 0)
@@ -198,11 +211,14 @@
             for c in downs:
                 c.wait_send()
 
-    first, rest = order[0], order[1:]
-    planes[0][0].wait()
-    each(odd, [down[first]], go)
-    for c in planes[0][1:] + planes[1] + others + planes[2]:
-        c.wait()
+    loaded(q.at[0, bottoms, own], 0)
+    each(odd, down[2:], go)
+    loaded(q.at[1:5, bottoms, own], 3)
+    loaded(q.at[:, tops, own], 1)
+    loaded(q.at[:, 2 : nx - 2, own], 2)
+    load(flags_in, flags, 4).wait()
+    loaded(dxz, 5)
+    loaded(dy.at[:, own], 6)
 
     flag = [flags[i].astype(jnp.float32) for i in range(6)]
 
@@ -242,21 +258,21 @@
     part[0:1] = jnp.sum(mass, 0, keepdims=True)
     part[1:2] = jnp.sum(power, 0, keepdims=True)
 
-    def message(src, dst, k, target):
+    def message(src, dst, ks, kr, target):
         return pltpu.make_async_remote_copy(
-            src_ref=src, dst_ref=dst, send_sem=sum_send.at[k], recv_sem=sum_recv.at[k],
+            src_ref=src, dst_ref=dst, send_sem=sum_send.at[ks], recv_sem=sum_recv.at[kr],
             device_id=target, device_id_type=mesh_ids,
         )
 
-    inward = message(part, slots.at[me * sz + last["gz"] - pos["gz"]], 0, {"gx": 0, "gz": last["gz"]})
-    gathered = message(slots.at[1:group], slots.at[1:group], 0, members[-1])
+    home = {"gx": 0, "gz": last["gz"]}
+    inward = message(part, slots.at[me * sz + last["gz"] - pos["gz"]], 0, 0, home)
+    gathered = message(slots.at[1:group], slots.at[1:group], 1, 0, members[-1])
     across = [
-        message(line.at[0], line.at[sy - o], 1, {"gy": lax.rem(pos["gy"] + o, sy)})
+        message(line.at[0], line.at[sy - o], 0, 1, {"gy": lax.rem(pos["gy"] + o, sy)})
         for o in range(1, sy)
     ]
-    crossed = message(line.at[1:sy], line.at[1:sy], 1, {"gy": lax.rem(pos["gy"] + 1, sy)})
-    outward = [message(done, done, 2, target) for target in members]
-    scattered = message(slots.at[1:group], slots.at[1:group], 2, members[-1])
+    crossed = message(line.at[1:sy], line.at[1:sy], 0, 1, {"gy": lax.rem(pos["gy"] + 1, sy)})
+    outward = [message(done, done, 1, 0, target) for target in members]
 
     each(~leader, [inward], go)
 
@@ -264,22 +280,21 @@
     each(below_y, y_down, go)
 
     def x_sends():
-        is_in(0, even & above_x)
-        each(even & below_x & above_x, [up[f] for f in direct], go)
-        is_in(1, me + 2 <= end)
-
-        @pl.when(even & (me + 2 <= end))
-        def _():
-            tell(in_sem.at[5], True, gx=me + 1)
-            tell(in_sem.at[5], True, gx=me + 2)
-
-        each(odd, [v_down] + [down[f] for f in rest], go)
-        each(odd & (me + 2 <= end), legs_up, go)
-        each(~below_x & above_x, [up[f] for f in direct], go)
-        is_in(5, hands_up | hands_down)
-        each(hands_up, [up[f] for f in direct] + [up_last], go)
-        each(hands_down, [v_down] + [down[f] for f in direct] + [down_last], go)
-        each(even & above_x, [up[f] for f in relayed + (4,)], go)
+        each(odd, [v_down] + down[:2], go)
+        waits = jnp.where(over, 1, 0) + jnp.where(above_x, 1, 0)
+        is_in(0, waits > 0, waits)
+
+        @pl.when(even & over)
+        def _():
+            tell(in_sem.at[0], True, gx=me + 1)
+            tell(in_sem.at[1], True, gx=me + 2)
+
+        each(even & above_x, up[:1], go)
+        each(odd & over, legs_up, go)
+        each(hands_up, up_across, go)
+        is_in(1, hands_down)
+        each(hands_down, [v_down] + down_across, go)
+        each(even & above_x, up[1:], go)
 
     pl.when(below_x | below_y)(x_sends)
 
@@ -299,10 +314,10 @@
     for k in range(parts):
         edge[k] = packed[k]
     each(below_z, z_down, go)
-    is_in(3, above_z)
+    beyond = jnp.where(above_y, 1, 0) + jnp.where(above_z, 1, 0)
+    is_in(2, beyond > 0, beyond)
     each(above_z, z_up, go)
     pl.when(~below_x & ~below_y)(x_sends)
-    is_in(2, above_y)
     each(above_y, y_up, go)
 
     outs = (
@@ -383,7 +398,7 @@
     def gather():
         gathered.wait_recv()
         line[0] = part[...] + jnp.sum(slots[1:group], 0)
-        is_in(4, pos["gy"] < last["gy"], last["gy"] - pos["gy"])
+        is_in(3, above_y, last["gy"] - pos["gy"])
         for c in across:
             c.start()
 
@@ -473,25 +488,19 @@
     def come(cond, copies):
         each(cond, copies, lambda c: c.wait_recv())
 
-    def lower(f):
-        come(odd, [up[f]])
-        if f in direct:
-            come(hands_down, [up[f]])
-        elif f in relayed:
-            come(hands_down, [handed_up[f - 1]])
-        else:
-            come(hands_down, [up_last, handed_up[2]])
-        rim(False, f)
-
-    def upper(f):
-        come(even & above_x, [down[f]])
-        if f in direct:
-            come(hands_up, [down[f]])
-        elif f in relayed:
-            come(hands_up, [handed_down[f - 1]])
-        else:
-            come(hands_up, [down_last, handed_down[2]])
-        rim(True, f)
+    def rims(high, i):
+        for f in ((3, 4), (1, 2), (0,))[i]:
+            rim(high, f)
+
+    def lower(i):
+        come(odd, [up[i]])
+        come(hands_down, ([up_across[0]], handed_up[:1], [up_across[1], handed_up[1]])[i])
+        rims(False, i)
+
+    def upper(i):
+        come(even & above_x, [down[i]])
+        come(hands_up, ([down_across[0]], handed_down[:1], [down_across[1], handed_down[1]])[i])
+        rims(True, i)
 
     def finish():
         crossed.wait_recv()
@@ -501,36 +510,33 @@
 
     @pl.when(hands_up)
     def _():
-        for f in direct:
-            upper(f)
-        for f in order:
-            lower(f)
-        for f in relayed + (4,):
-            upper(f)
+        upper(0)
+        for i in range(3):
+            lower(i)
+        upper(1)
+        upper(2)
 
     @pl.when(odd & ~above_x)
     def _():
-        for f in order:
-            upper(f)
-        for f in order:
-            lower(f)
+        for i in range(3):
+            upper(i)
+        for i in range(3):
+            lower(i)
 
     @pl.when(hands_down)
     def _():
-        for f in order:
-            upper(f)
-        for f in order:
-            lower(f)
+        for i in (2, 0, 1):
+            upper(i)
+        for i in range(3):
+            lower(i)
 
     @pl.when(~below_x)
     def _():
-        for f in order:
-            lower(f)
-        for f in direct:
-            upper(f)
+        for i in range(3):
+            lower(i)
         pl.when(leader)(finish)
-        for f in relayed + (4,):
-            upper(f)
+        for i in (2, 0, 1):
+            upper(i)
 
     @pl.when(~leader)
     def _():
@@ -542,40 +548,37 @@
     @pl.when(leader)
     def _():
         crossed.wait_send()
-        scattered.wait_send()
-
-    def sent(cond, copies):
+        gathered.wait_send()
+
+    def sent(k, cond, ref):
+        @pl.when(cond)
+        def _():
+            copy(k, 0, ref, ref, "gx", 1 - 2 * par).wait_send()
+
+    sent(main, even & above_x | odd, xlo)
+    sent(2, below_x, xv)
+    five = q.at[:, 0, own]
+    sent(across_x, hands_up | hands_down, five)
+    sent(legs_k, odd & over | hands_down, five)
+    sent(hand_k, relays, five)
+    for cond, copies in ((above_y, y_up), (below_y, y_down), (above_z, z_up), (below_z, z_down)):
         each(cond, copies, lambda c: c.wait_send())
 
-    sent(below_x, [v_down] + [down[f] for f in direct])
-    sent(odd, [down[f] for f in relayed + (4,)])
-    sent(above_x, [up[f] for f in direct])
-    sent(even & above_x, [up[f] for f in relayed + (4,)])
-    sent(hands_up, [up_last])
-    sent(hands_down, [down_last])
-    sent(odd & (me + 2 <= end), legs_up)
-    sent(hands_down, legs_down)
-    sent(relays & odd, handed_up)
-    sent(relays & even, handed_down)
-    sent(above_y, y_up)
-    sent(below_y, y_down)
-    sent(above_z, z_up)
-    sent(below_z, z_down)
-
 
 def put(cells, den, mom, en, sums, out_d, out_m, out_e, totals, mean, sem):
-    pairs = ((mom, out_m), (den, out_d), (en, out_e))
-    moves = [
-        pltpu.make_async_copy(src, dst, sem.at[i]) for i, (src, dst) in enumerate(pairs)
-    ]
-    for c in moves:
-        c.start()
+    half = den.shape[0] // 2
+    pairs = ((den, out_d), (en, out_e), (mom, out_m))
+    for i, (src, dst) in enumerate(pairs):
+        for h in (pl.ds(0, half), pl.ds(half, den.shape[0] - half)):
+            for at in ((h,),) if i < 2 else tuple((c, h) for c in range(3)):
+                pltpu.make_async_copy(src.at[at], dst.at[at], sem.at[i]).start()
     mean[0] = jnp.sum(sums[0:1]) / cells
     mean[1] = jnp.sum(sums[1:2]) / cells
-    moves.append(pltpu.make_async_copy(mean, totals, sem.at[3]))
-    moves[-1].start()
-    for c in moves:
-        c.wait()
+    last = pltpu.make_async_copy(mean, totals, sem.at[3])
+    last.start()
+    for i, (src, dst) in enumerate(pairs):
+        pltpu.make_async_copy(src, dst, sem.at[i]).wait()
+    last.wait()
 
 
 def shards(density, momentum, energy, displacement, flags):
@@ -602,17 +605,16 @@
         scratch_shapes=[
             pltpu.SMEM((6,), i32),
             pltpu.VMEM((5, nx, tall, nz), f32),
-            pltpu.VMEM((nx, ny, nz), i32),
+            pltpu.VMEM((2, nx, ny, nz), i32),
             pltpu.VMEM((nx, tall, nz), i32),
-            pltpu.VMEM((nx, ny, nz), i32),
             pltpu.VMEM((2, 5, 2, ny, nz), f32),
-            pltpu.VMEM((5, ny, nz), f32),
+            pltpu.VMEM((3, 2, ny, nz), f32),
             pltpu.VMEM((ny, nz), i32),
         ]
         + [pltpu.VMEM((parts, ny, nz), f32) for _ in range(5)]
         + [pltpu.VMEM((2, nz), f32), pltpu.VMEM((sizes["gx"] * sizes["gz"], 2, nz), f32)]
         + [pltpu.VMEM((sizes["gy"], 2, nz), f32), pltpu.VMEM((2, nz), f32)]
-        + [dma((13,)), dma((26,)), dma((26,)), pltpu.SemaphoreType.REGULAR((6,)), dma((3,)), dma((3,))],
+        + [dma((7,)), dma((10,)), dma((16,)), pltpu.SemaphoreType.REGULAR((4,)), dma((2,)), dma((2,))],
         compiler_params=pltpu.CompilerParams(
             collective_id=0, has_side_effects=True, vmem_limit_bytes=12 << 20
         ),

time: 17.4 us -> 16.9 us (0.971)
  Pallas kernels: 16.6 us -> 16.1 us
    pallas_call x1, Pallas kernels: 15.5 us -> 15.1 us  [shards(): pl.pallas_call(functools.partial(kernel, sizes), out_shape=outputs + (jax...]
where the time goes in v3:
time: 16.9 us; the launch traced here: 16.8 us
  Pallas kernels  16.1 us (95%)
  between operations  0.64 us (4%)
    pallas_call x1, Pallas kernels, shards(): pl.pallas_call(functools.partial(kernel, sizes), out_shape=outputs + (jax...  15.1 us
    pallas_call x1, Pallas kernels, shards(): pl.pallas_call(functools.partial(put, cells), out_shape=outputs + (jax.Sh...  1.09 us

profile of v3, /device:TPU:5, one launch (start us, length us, event | category | flops | bytes accessed | tf_op | source)
XLA Modules:
  0.0 16.8 jit_solution(8997610677377406775)
XLA Ops:
  0.6 15.1 %shard_map.84 = (f32[8,64,128]{2,1,0:T(8,128)S(1)}, f32[3,8,64,128]{3,2,1,0:T(8,128)S(1)}, f32[8,64,128]{2,1,0:T(8,128)S(1)}, f32[2,128]{1,0:T(2,128)S(1)}) custom-call(s32[6]{0:T(128)} %flags_in.1, f32[8,64,128]{2,1,0:T(8,128)} %den.1, f32[3,8,64,128]{3,2,1,0:T(8,128)} %mom.1, f32[8,64,128]{2,1,0:T(8,128)} %en.1, s32[3,8,64,128]{3,2,1,0:T(8,128)} %disp.1), custom_call_target="tpu_custom_call" | custom-call | tf_op jit(solution)/shard_map/pallas_call | solution.py:600
  15.7 1.1 %shard_map.85 = (f32[8,64,128]{2,1,0:T(8,128)}, f32[3,8,64,128]{3,2,1,0:T(8,128)}, f32[8,64,128]{2,1,0:T(8,128)}, f32[2]{0:T(128)}) custom-call(f32[8,64,128]{2,1,0:T(8,128)S(1)} %get-tuple-element.8.den, f32[3,8,64,128]{3,2,1,0:T(8,128)S(1)} %get-tuple-element.9.mom, f32[8,64,128]{2,1,0:T(8,128)S(1)} %get-tuple-element.10.en, ...), custom_call_target="tpu_custom_call" | custom-call | tf_op jit(solution)/shard_map/pallas_call | solution.py:627

commit v4 on v3

--- a/solution.py
+++ b/solution.py
@@ -28,7 +28,7 @@
 def kernel(
     sizes, flags_in, den, mom, en, disp, out_d, out_m, out_e, sums,
     flags, q, dxz, dy, xh, hop, xv, edge, zlo, zhi, cq, cs, part, slots, line, done,
-    local_sem, send_sem, recv_sem, in_sem, sum_send, sum_recv,
+    send_sem, recv_sem, in_sem, sum_send, sum_recv,
 ):
     nx, ny, nz = den.shape
     pos = {a: lax.axis_index(a) for a in AXES}
@@ -43,7 +43,7 @@
     mesh_ids = pl.DeviceIdType.MESH
 
     def load(src, dst, k):
-        return pltpu.make_async_copy(src, dst, local_sem.at[k])
+        return pltpu.make_async_copy(src, dst, send_sem.at[k])
 
     spans = (slice(0, 2), slice(nx - 2, nx), slice(2, nx - 2))
     loads = []
@@ -148,17 +148,17 @@
     down_across = [piece(across_x, 0, bottoms, xhi, 3, -1), one(across_x, 5, 1, xhi, 1, -1)]
     legs_up = [
         copy(legs_k, 7, q.at[1:3, tops, own], hop.at[0:2], "gx", 2),
-        copy(legs_k, 8, q.at[0, nx - 2, own], hop.at[2, 0], "gx", 2),
+        copy(legs_k, 7, q.at[0, nx - 2, own], hop.at[2, 0], "gx", 2),
     ]
     legs_down = [
         copy(legs_k, 7, q.at[1:3, bottoms, own], hop.at[0:2], "gx", -2),
-        copy(legs_k, 8, q.at[0, 0, own], hop.at[2, 0], "gx", -2),
+        copy(legs_k, 7, q.at[0, 0, own], hop.at[2, 0], "gx", -2),
     ]
 
     def handed(side):
         return [
-            copy(hand_k, 9, hop.at[0:2], side.at[1:3], "gx", beside),
-            copy(hand_k, 10, hop.at[2, 0], side.at[0, 0], "gx", beside),
+            copy(hand_k, 8, hop.at[0:2], side.at[1:3], "gx", beside),
+            copy(hand_k, 9, hop.at[2, 0], side.at[0, 0], "gx", beside),
         ]
 
     handed_up, handed_down = handed(xlo), handed(xhi)
@@ -173,13 +173,14 @@
         c.start()
 
     hi_rows = slice(top, top + SUB)
-    y_up = [copy(5, 11, q.at[:, :, ny:top], q.at[:, :, 0:SUB], "gy", 1)]
+    y_up = [copy(5, 10, q.at[:, :, ny:top], q.at[:, :, 0:SUB], "gy", 1)]
     y_down = [
-        copy(6, 12, q.at[:, :, SUB : 2 * SUB], q.at[:, :, hi_rows], "gy", -1),
-        copy(7, 13, dy.at[:, SUB : 2 * SUB], dy.at[:, hi_rows], "gy", -1),
+        copy(6, 11, q.at[:, :, SUB : 2 * SUB], q.at[:, :, hi_rows], "gy", -1),
+        copy(7, 12, dy.at[:, SUB : 2 * SUB], dy.at[:, hi_rows], "gy", -1),
     ]
-    z_up = [copy(8, 14, edge, zlo, "gz", 1)]
-    z_down = [copy(9, 15, edge, zhi, "gz", -1)]
+    both = sz > 2
+    z_up = [copy(8, 13, edge, zlo, "gz", 1)]
+    z_down = [copy(8 + both, 13 + both, edge, zhi, "gz", -1)]
 
     def arrive(axis, ups, downs, fill_low, fill_high):
         @pl.when(pos[axis] > 0)
@@ -405,15 +406,12 @@
     pl.when(leader & below_y)(gather)
     lax.fori_loop(early, nx, along_z, 0)
 
-    def hand_on(cond, legs, onward):
-        @pl.when(relays & cond)
-        def _():
-            for a, b in zip(legs, onward):
-                a.wait_recv()
-                b.start()
-
-    hand_on(odd, legs_up, handed_up)
-    hand_on(even, legs_down, handed_down)
+    @pl.when(relays)
+    def _():
+        copy(legs_k, 7, q.at[:, 0, own], q.at[:, 0, own], "gx", beside).wait_recv()
+
+    each(relays & odd, handed_up, go)
+    each(relays & even, handed_down, go)
 
     def y_low():
         q[:, :, 0:SUB] = jnp.broadcast_to(q[:, :, SUB : SUB + 1], (5, nx, SUB, nz))
@@ -458,10 +456,12 @@
     each(above_x, [v_down], lambda c: c.wait_recv())
     x_lo_mult, x_hi_mult = low_mult(0) * scale, high_mult(0) * scale
 
+    tile = 4 * SUB if ny % (4 * SUB) == 0 else SUB
+
     def rim(high, f):
         def rows(r, _):
-            at = pl.ds(pl.multiple_of(r * SUB, SUB), SUB)
-            inner = pl.ds(pl.multiple_of(r * SUB + SUB, SUB), SUB)
+            at = pl.ds(pl.multiple_of(r * tile, SUB), tile)
+            inner = pl.ds(pl.multiple_of(r * tile + SUB, SUB), tile)
             if high:
                 cells = [q[f, c, inner] for c in range(nx - 3, nx)] + [xhi[f, i, at] for i in range(2)]
                 vs = (dx[nx - 1, at].astype(jnp.float32) * scale, xv[at].astype(jnp.float32) * x_hi_mult)
@@ -483,7 +483,7 @@
                 ref[at] += change
             return 0
 
-        lax.fori_loop(0, ny // SUB, rows, 0)
+        lax.fori_loop(0, ny // tile, rows, 0)
 
     def come(cond, copies):
         each(cond, copies, lambda c: c.wait_recv())
@@ -508,35 +508,22 @@
         for c in outward:
             c.start()
 
-    @pl.when(hands_up)
-    def _():
-        upper(0)
-        for i in range(3):
-            lower(i)
-        upper(1)
-        upper(2)
-
-    @pl.when(odd & ~above_x)
-    def _():
-        for i in range(3):
-            upper(i)
-        for i in range(3):
-            lower(i)
-
-    @pl.when(hands_down)
-    def _():
-        for i in (2, 0, 1):
-            upper(i)
-        for i in range(3):
-            lower(i)
-
-    @pl.when(~below_x)
-    def _():
-        for i in range(3):
-            lower(i)
-        pl.when(leader)(finish)
-        for i in (2, 0, 1):
-            upper(i)
+    pl.when(leader)(finish)
+
+    def sides(turn, _):
+        @pl.when((turn == 1) == hands_up)
+        def _():
+            for i in (2, 0, 1):
+                upper(i)
+
+        @pl.when(turn == 0)
+        def _():
+            for i in range(3):
+                lower(i)
+
+        return 0
+
+    lax.fori_loop(0, 2, sides, 0)
 
     @pl.when(~leader)
     def _():
@@ -614,7 +601,7 @@
         + [pltpu.VMEM((parts, ny, nz), f32) for _ in range(5)]
         + [pltpu.VMEM((2, nz), f32), pltpu.VMEM((sizes["gx"] * sizes["gz"], 2, nz), f32)]
         + [pltpu.VMEM((sizes["gy"], 2, nz), f32), pltpu.VMEM((2, nz), f32)]
-        + [dma((7,)), dma((10,)), dma((16,)), pltpu.SemaphoreType.REGULAR((4,)), dma((2,)), dma((2,))],
+        + [dma((9 + (sizes["gz"] > 2),)), dma((14 + (sizes["gz"] > 2),)), pltpu.SemaphoreType.REGULAR((4,)), dma((2,)), dma((2,))],
         compiler_params=pltpu.CompilerParams(
             collective_id=0, has_side_effects=True, vmem_limit_bytes=12 << 20
         ),

time: 16.9 us -> 16.8 us (level)
  no operation moved by 1% of the time
where the time goes in v4:
time: 16.8 us; the launch traced here: 16.7 us
  Pallas kernels  16 us (95%)
  between operations  0.64 us (4%)
    pallas_call x1, Pallas kernels, shards(): pl.pallas_call(functools.partial(kernel, sizes), out_shape=outputs + (jax...  14.9 us
    pallas_call x1, Pallas kernels, shards(): pl.pallas_call(functools.partial(put, cells), out_shape=outputs + (jax.Sh...  1.09 us

profile of v4, /device:TPU:5, one launch (start us, length us, event | category | flops | bytes accessed | tf_op | source)
XLA Modules:
  0.0 16.7 jit_solution(5123198668861110263)
XLA Ops:
  0.6 14.9 %shard_map.84 = (f32[8,64,128]{2,1,0:T(8,128)S(1)}, f32[3,8,64,128]{3,2,1,0:T(8,128)S(1)}, f32[8,64,128]{2,1,0:T(8,128)S(1)}, f32[2,128]{1,0:T(2,128)S(1)}) custom-call(s32[6]{0:T(128)} %flags_in.1, f32[8,64,128]{2,1,0:T(8,128)} %den.1, f32[3,8,64,128]{3,2,1,0:T(8,128)} %mom.1, f32[8,64,128]{2,1,0:T(8,128)} %en.1, s32[3,8,64,128]{3,2,1,0:T(8,128)} %disp.1), custom_call_target="tpu_custom_call" | custom-call | tf_op jit(solution)/shard_map/pallas_call | solution.py:587
  15.6 1.1 %shard_map.85 = (f32[8,64,128]{2,1,0:T(8,128)}, f32[3,8,64,128]{3,2,1,0:T(8,128)}, f32[8,64,128]{2,1,0:T(8,128)}, f32[2]{0:T(128)}) custom-call(f32[8,64,128]{2,1,0:T(8,128)S(1)} %get-tuple-element.8.den, f32[3,8,64,128]{3,2,1,0:T(8,128)S(1)} %get-tuple-element.9.mom, f32[8,64,128]{2,1,0:T(8,128)S(1)} %get-tuple-element.10.en, ...), custom_call_target="tpu_custom_call" | custom-call | tf_op jit(solution)/shard_map/pallas_call | solution.py:614

commit v5 on v4

--- a/solution.py
+++ b/solution.py
@@ -25,8 +25,16 @@
     return v * jnp.where(up, q_low, q_high) + g * jnp.where(up, s_low, s_high)
 
 
+def rim_fluxes(line_q, vs):
+    ds = [line_q[i + 1] - line_q[i] for i in range(4)]
+    ss = [minmod(ds[i + 1], ds[i]) for i in range(3)]
+    return [
+        flux(vs[i], gain(vs[i]), line_q[i + 1], line_q[i + 2], ss[i], ss[i + 1]) for i in range(2)
+    ]
+
+
 def kernel(
-    sizes, flags_in, den, mom, en, disp, out_d, out_m, out_e, sums,
+    sizes, flags_in, den, mom, en, disp, out_d, out_m, out_e, sums, ghost, cells,
     flags, q, dxz, dy, xh, hop, xv, edge, zlo, zhi, cq, cs, part, slots, line, done,
     send_sem, recv_sem, in_sem, sum_send, sum_recv,
 ):
@@ -47,17 +55,17 @@
 
     spans = (slice(0, 2), slice(nx - 2, nx), slice(2, nx - 2))
     loads = []
-    for i, x in enumerate(spans):
+    for x, k, first in zip(spans, (1, 2, 2), (0, 2, 2)):
         loads += [
-            load(den.at[x], q.at[0, x, own], i),
-            load(en.at[x], q.at[4, x, own], max(i, 3 - 3 * i)),
-            load(mom.at[:, x], q.at[1:4, x, own], max(i, 3 - 3 * i)),
+            load(den.at[x], q.at[0, x, own], first),
+            load(en.at[x], q.at[4, x, own], k),
+            load(mom.at[:, x], q.at[1:4, x, own], k),
         ]
     loads += [
-        load(flags_in, flags, 4),
-        load(disp.at[0], dx, 5),
-        load(disp.at[2], dz, 5),
-        load(disp.at[1], dy.at[:, own], 6),
+        load(flags_in, flags, 3),
+        load(disp.at[0], dx, 4),
+        load(disp.at[2], dz, 4),
+        load(disp.at[1], dy.at[:, own], 5),
     ]
     for c in loads:
         c.start()
@@ -129,36 +137,39 @@
     hands_up, hands_down = odd & above_x, inner
     relays = (odd & (me >= 3)) | (even & over)
     beside = 1 - 2 * par
-    main, across_x, legs_k, hand_k = 0, 1, 3, 4
+    main, hand_k = 0, 1
 
     groups = (slice(3, 5), slice(1, 3), 0)
     tops, bottoms = slice(nx - 2, nx), slice(0, 2)
 
+    def dst(side, f):
+        return ghost if side is xlo and f == 0 else side.at[f]
+
     def piece(k, i, x, side, first, step):
         f = groups[i]
-        return copy(k, first + i, q.at[f, x, own], side.at[f], "gx", step)
+        return copy(k, first + i, q.at[f, x, own], dst(side, f), "gx", step)
 
     def one(k, r, x, side, i, step):
-        return copy(k, r, q.at[0, x, own], side.at[0, i], "gx", step)
+        return copy(k, r, q.at[0, x, own], dst(side, 0).at[i], "gx", step)
 
     up = [piece(main, i, tops, xlo, 0, 1) for i in range(3)]
     down = [piece(main, i, bottoms, xhi, 3, -1) for i in range(3)]
     v_down = copy(2, 6, dx.at[0], xv, "gx", -1)
-    up_across = [piece(across_x, 0, tops, xlo, 0, 1), one(across_x, 2, nx - 1, xlo, 1, 1)]
-    down_across = [piece(across_x, 0, bottoms, xhi, 3, -1), one(across_x, 5, 1, xhi, 1, -1)]
+    up_across = [piece(main, 0, tops, xlo, 0, 1), one(main, 2, nx - 1, xlo, 1, 1)]
+    down_across = [piece(main, 0, bottoms, xhi, 3, -1), one(main, 5, 1, xhi, 1, -1)]
     legs_up = [
-        copy(legs_k, 7, q.at[1:3, tops, own], hop.at[0:2], "gx", 2),
-        copy(legs_k, 7, q.at[0, nx - 2, own], hop.at[2, 0], "gx", 2),
+        copy(main, 7, q.at[1:3, tops, own], hop.at[0:2], "gx", 2),
+        copy(main, 7, q.at[0, nx - 2, own], hop.at[2, 0], "gx", 2),
     ]
     legs_down = [
-        copy(legs_k, 7, q.at[1:3, bottoms, own], hop.at[0:2], "gx", -2),
-        copy(legs_k, 7, q.at[0, 0, own], hop.at[2, 0], "gx", -2),
+        copy(main, 7, q.at[1:3, bottoms, own], hop.at[0:2], "gx", -2),
+        copy(main, 7, q.at[0, 0, own], hop.at[2, 0], "gx", -2),
     ]
 
     def handed(side):
         return [
             copy(hand_k, 8, hop.at[0:2], side.at[1:3], "gx", beside),
-            copy(hand_k, 9, hop.at[2, 0], side.at[0, 0], "gx", beside),
+            copy(hand_k, 9, hop.at[2, 0], dst(side, 0).at[0], "gx", beside),
         ]
 
     handed_up, handed_down = handed(xlo), handed(xhi)
@@ -173,14 +184,14 @@
         c.start()
 
     hi_rows = slice(top, top + SUB)
-    y_up = [copy(5, 10, q.at[:, :, ny:top], q.at[:, :, 0:SUB], "gy", 1)]
+    y_up = [copy(3, 10, q.at[:, :, ny:top], q.at[:, :, 0:SUB], "gy", 1)]
     y_down = [
-        copy(6, 11, q.at[:, :, SUB : 2 * SUB], q.at[:, :, hi_rows], "gy", -1),
-        copy(7, 12, dy.at[:, SUB : 2 * SUB], dy.at[:, hi_rows], "gy", -1),
+        copy(3, 11, q.at[:, :, SUB : 2 * SUB], q.at[:, :, hi_rows], "gy", -1),
+        copy(4, 12, dy.at[:, SUB : 2 * SUB], dy.at[:, hi_rows], "gy", -1),
     ]
     both = sz > 2
-    z_up = [copy(8, 13, edge, zlo, "gz", 1)]
-    z_down = [copy(8 + both, 13 + both, edge, zhi, "gz", -1)]
+    z_up = [copy(5, 13, edge, zlo, "gz", 1)]
+    z_down = [copy(5 + both, 13 + both, edge, zhi, "gz", -1)]
 
     def arrive(axis, ups, downs, fill_low, fill_high):
         @pl.when(pos[axis] > 0)
@@ -214,12 +225,11 @@
 
     loaded(q.at[0, bottoms, own], 0)
     each(odd, down[2:], go)
-    loaded(q.at[1:5, bottoms, own], 3)
-    loaded(q.at[:, tops, own], 1)
-    loaded(q.at[:, 2 : nx - 2, own], 2)
-    load(flags_in, flags, 4).wait()
-    loaded(dxz, 5)
-    loaded(dy.at[:, own], 6)
+    loaded(q.at[1:5, bottoms, own], 1)
+    loaded(q.at[:, 2:nx, own], 2)
+    load(flags_in, flags, 3).wait()
+    loaded(dxz, 4)
+    loaded(dy.at[:, own], 5)
 
     flag = [flags[i].astype(jnp.float32) for i in range(6)]
 
@@ -408,7 +418,7 @@
 
     @pl.when(relays)
     def _():
-        copy(legs_k, 7, q.at[:, 0, own], q.at[:, 0, own], "gx", beside).wait_recv()
+        copy(hand_k, 7, q.at[:, 0, own], q.at[:, 0, own], "gx", beside).wait_recv()
 
     each(relays & odd, handed_up, go)
     each(relays & even, handed_down, go)
@@ -447,6 +457,7 @@
     @pl.when(me == 0)
     def _():
         xlo[...] = jnp.broadcast_to(q[:, 0:1, own], (5, 2, ny, nz))
+        ghost[...] = jnp.broadcast_to(q[0, 0:1, own], (2, ny, nz))
 
     @pl.when(me == end)
     def _():
@@ -457,23 +468,22 @@
     x_lo_mult, x_hi_mult = low_mult(0) * scale, high_mult(0) * scale
 
     tile = 4 * SUB if ny % (4 * SUB) == 0 else SUB
+
+    cells[0:3] = q[0, 0:3, own]
+    cells[3] = dx[0].astype(jnp.float32) * x_lo_mult
+    cells[4] = dx[1].astype(jnp.float32) * scale
 
     def rim(high, f):
         def rows(r, _):
             at = pl.ds(pl.multiple_of(r * tile, SUB), tile)
             inner = pl.ds(pl.multiple_of(r * tile + SUB, SUB), tile)
             if high:
-                cells = [q[f, c, inner] for c in range(nx - 3, nx)] + [xhi[f, i, at] for i in range(2)]
+                line_q = [q[f, c, inner] for c in range(nx - 3, nx)] + [xhi[f, i, at] for i in range(2)]
                 vs = (dx[nx - 1, at].astype(jnp.float32) * scale, xv[at].astype(jnp.float32) * x_hi_mult)
             else:
-                cells = [xlo[f, i, at] for i in range(2)] + [q[f, c, inner] for c in range(3)]
+                line_q = [xlo[f, i, at] for i in range(2)] + [q[f, c, inner] for c in range(3)]
                 vs = (dx[0, at].astype(jnp.float32) * x_lo_mult, dx[1, at].astype(jnp.float32) * scale)
-            ds = [cells[i + 1] - cells[i] for i in range(4)]
-            ss = [minmod(ds[i + 1], ds[i]) for i in range(3)]
-            fl = [
-                flux(vs[i], gain(vs[i]), cells[i + 1], cells[i + 2], ss[i], ss[i + 1])
-                for i in range(2)
-            ]
+            fl = rim_fluxes(line_q, vs)
             if high:
                 changes = ((nx - 2, -fl[0]), (nx - 1, fl[0] - fl[1]))
             else:
@@ -495,7 +505,8 @@
     def lower(i):
         come(odd, [up[i]])
         come(hands_down, ([up_across[0]], handed_up[:1], [up_across[1], handed_up[1]])[i])
-        rims(False, i)
+        if i < 2:
+            rims(False, i)
 
     def upper(i):
         come(even & above_x, [down[i]])
@@ -540,32 +551,50 @@
     def sent(k, cond, ref):
         @pl.when(cond)
         def _():
-            copy(k, 0, ref, ref, "gx", 1 - 2 * par).wait_send()
-
-    sent(main, even & above_x | odd, xlo)
+            copy(k, 0, ref, ref, "gx", beside).wait_send()
+
+    pair = hands_up | hands_down
+    sent(main, pair, xh)
+    sent(main, ~pair, xlo)
+    sent(hand_k, relays, q.at[:, 0, own])
     sent(2, below_x, xv)
-    five = q.at[:, 0, own]
-    sent(across_x, hands_up | hands_down, five)
-    sent(legs_k, odd & over | hands_down, five)
-    sent(hand_k, relays, five)
-    for cond, copies in ((above_y, y_up), (below_y, y_down), (above_z, z_up), (below_z, z_down)):
-        each(cond, copies, lambda c: c.wait_send())
-
-
-def put(cells, den, mom, en, sums, out_d, out_m, out_e, totals, mean, sem):
-    half = den.shape[0] // 2
-    pairs = ((den, out_d), (en, out_e), (mom, out_m))
-    for i, (src, dst) in enumerate(pairs):
-        for h in (pl.ds(0, half), pl.ds(half, den.shape[0] - half)):
-            for at in ((h,),) if i < 2 else tuple((c, h) for c in range(3)):
-                pltpu.make_async_copy(src.at[at], dst.at[at], sem.at[i]).start()
-    mean[0] = jnp.sum(sums[0:1]) / cells
-    mean[1] = jnp.sum(sums[1:2]) / cells
-    last = pltpu.make_async_copy(mean, totals, sem.at[3])
-    last.start()
-    for i, (src, dst) in enumerate(pairs):
-        pltpu.make_async_copy(src, dst, sem.at[i]).wait()
-    last.wait()
+    sent(3, above_y & below_y, q.at[:, :, 0 : 2 * SUB])
+    sent(3, above_y ^ below_y, q.at[:, :, 0:SUB])
+    sent(4, below_y, dy.at[:, 0:SUB])
+    sent(5, above_z, edge)
+    sent(5 + both, below_z, edge)
+
+
+def put(count, den, mom, en, sums, ghost, cells, out_d, out_m, out_e, totals, edge, mean, sem):
+    nx = den.shape[0]
+    half = nx // 2
+    moves = [
+        (den.at[2:nx], out_d.at[2:nx], 0),
+        (en.at[0:half], out_e.at[0:half], 1),
+        (en.at[half:nx], out_e.at[half:nx], 1),
+    ]
+    for c in range(3):
+        moves += [(mom.at[c, h], out_m.at[c, h], 2) for h in (pl.ds(0, half), pl.ds(half, nx - half))]
+    for src, dst, k in moves:
+        pltpu.make_async_copy(src, dst, sem.at[k]).start()
+
+    line_q = [ghost[0], ghost[1]] + [cells[c] for c in range(3)]
+    fl = rim_fluxes(line_q, (cells[3], cells[4]))
+    edge[0] = den[0] + (fl[0] - fl[1])
+    edge[1] = den[1] + fl[1]
+    mean[0] = jnp.sum(sums[0:1]) / count
+    mean[1] = jnp.sum(sums[1:2]) / count
+    rest = [
+        pltpu.make_async_copy(mean, totals, sem.at[3]),
+        pltpu.make_async_copy(edge, out_d.at[0:2], sem.at[4]),
+    ]
+    for c in rest:
+        c.start()
+    pltpu.make_async_copy(den.at[2:nx], out_d.at[2:nx], sem.at[0]).wait()
+    pltpu.make_async_copy(en, out_e, sem.at[1]).wait()
+    pltpu.make_async_copy(mom, out_m, sem.at[2]).wait()
+    for c in rest:
+        c.wait()
 
 
 def shards(density, momentum, energy, displacement, flags):
@@ -582,13 +611,15 @@
     devices = 1
     for a in AXES:
         devices *= sizes[a]
-    cells = float(nx * ny * nz * devices)
+    count = float(nx * ny * nz * devices)
     outputs = tuple(jax.ShapeDtypeStruct(v.shape, f32) for v in (density, momentum, energy))
     results = pl.pallas_call(
         functools.partial(kernel, sizes),
-        out_shape=outputs + (jax.ShapeDtypeStruct((2, nz), f32),),
+        out_shape=outputs + tuple(
+            jax.ShapeDtypeStruct(v, f32) for v in ((2, nz), (2, ny, nz), (5, ny, nz))
+        ),
         in_specs=[hbm] * 5,
-        out_specs=(vmem, vmem, vmem, vmem),
+        out_specs=(vmem,) * 6,
         scratch_shapes=[
             pltpu.SMEM((6,), i32),
             pltpu.VMEM((5, nx, tall, nz), f32),
@@ -601,7 +632,7 @@
         + [pltpu.VMEM((parts, ny, nz), f32) for _ in range(5)]
         + [pltpu.VMEM((2, nz), f32), pltpu.VMEM((sizes["gx"] * sizes["gz"], 2, nz), f32)]
         + [pltpu.VMEM((sizes["gy"], 2, nz), f32), pltpu.VMEM((2, nz), f32)]
-        + [dma((9 + (sizes["gz"] > 2),)), dma((14 + (sizes["gz"] > 2),)), pltpu.SemaphoreType.REGULAR((4,)), dma((2,)), dma((2,))],
+        + [dma((6 + (sizes["gz"] > 2),)), dma((14 + (sizes["gz"] > 2),)), pltpu.SemaphoreType.REGULAR((4,)), dma((2,)), dma((2,))],
         compiler_params=pltpu.CompilerParams(
             collective_id=0, has_side_effects=True, vmem_limit_bytes=12 << 20
         ),
@@ -612,11 +643,11 @@
         )
     )
     return pl.pallas_call(
-        functools.partial(put, cells),
+        functools.partial(put, count),
         out_shape=outputs + (jax.ShapeDtypeStruct((2,), f32),),
-        in_specs=[any_, any_, any_, vmem],
+        in_specs=[vmem, any_, any_, vmem, vmem, vmem],
         out_specs=(hbm, hbm, hbm, hbm),
-        scratch_shapes=[pltpu.SMEM((2,), f32), dma((4,))],
+        scratch_shapes=[pltpu.VMEM((2, ny, nz), f32), pltpu.SMEM((2,), f32), dma((5,))],
         compiler_params=pltpu.CompilerParams(vmem_limit_bytes=2 << 20),
     )(*results)
 

time: 16.8 us -> 16.7 us (level)
  no operation moved by 1% of the time
where the time goes in v5:
time: 16.7 us; the launch traced here: 16.5 us
  Pallas kernels  15.9 us (95%)
  between operations  0.64 us (4%)
    pallas_call x1, Pallas kernels, shards(): pl.pallas_call(functools.partial(kernel, sizes), out_shape=outputs + tupl...  14.8 us
    pallas_call x1, Pallas kernels, shards(): pl.pallas_call(functools.partial(put, count), out_shape=outputs + (jax.Sh...  1.08 us

profile of v5, /device:TPU:5, one launch (start us, length us, event | category | flops | bytes accessed | tf_op | source)
XLA Modules:
  0.0 16.5 jit_solution(6766810814594614903)
XLA Ops:
  0.6 14.8 %shard_map.84 = (f32[8,64,128]{2,1,0:T(8,128)S(1)}, f32[3,8,64,128]{3,2,1,0:T(8,128)S(1)}, f32[8,64,128]{2,1,0:T(8,128)S(1)}, f32[2,128]{1,0:T(2,128)S(1)}, f32[...) custom-call(s32[6]{0:T(128)} %flags_in.1, f32[8,64,128]{2,1,0:T(8,128)} %den.1, f32[3,8,64,128]{3,2,1,0:T(8,128)} %mom.1, ...), custom_call_target="tpu_custom_call" | custom-call | tf_op jit(solution)/shard_map/pallas_call | solution.py:616
  15.4 1.1 %shard_map.85 = (f32[8,64,128]{2,1,0:T(8,128)}, f32[3,8,64,128]{3,2,1,0:T(8,128)}, f32[8,64,128]{2,1,0:T(8,128)}, f32[2]{0:T(128)}) custom-call(f32[8,64,128]{2,1,0:T(8,128)S(1)} %get-tuple-element.10.den, f32[3,8,64,128]{3,2,1,0:T(8,128)S(1)} %get-tuple-element.11.mom, f32[8,64,128]{2,1,0:T(8,128)S(1)} %get-tuple-element.12.en, ...), custom_call_target="tpu_custom_call" | custom-call | tf_op jit(solution)/shard_map/pallas_call | solution.py:645

commit v6 on v5

--- a/solution.py
+++ b/solution.py
@@ -521,48 +521,49 @@
 
     pl.when(leader)(finish)
 
-    def sides(turn, _):
-        @pl.when((turn == 1) == hands_up)
-        def _():
-            for i in (2, 0, 1):
-                upper(i)
-
-        @pl.when(turn == 0)
-        def _():
-            for i in range(3):
-                lower(i)
-
-        return 0
-
-    lax.fori_loop(0, 2, sides, 0)
-
-    @pl.when(~leader)
-    def _():
-        outward[0].wait_recv()
-        inward.wait_send()
-
-    sums[...] = done[...]
-
-    @pl.when(leader)
-    def _():
-        crossed.wait_send()
-        gathered.wait_send()
-
     def sent(k, cond, ref):
         @pl.when(cond)
         def _():
             copy(k, 0, ref, ref, "gx", beside).wait_send()
 
-    pair = hands_up | hands_down
-    sent(main, pair, xh)
-    sent(main, ~pair, xlo)
-    sent(hand_k, relays, q.at[:, 0, own])
     sent(2, below_x, xv)
     sent(3, above_y & below_y, q.at[:, :, 0 : 2 * SUB])
     sent(3, above_y ^ below_y, q.at[:, :, 0:SUB])
     sent(4, below_y, dy.at[:, 0:SUB])
     sent(5, above_z, edge)
     sent(5 + both, below_z, edge)
+    each(~leader, [inward], lambda c: c.wait_send())
+    each(leader, [crossed], lambda c: c.wait_send())
+
+    def sides(turn, _):
+        @pl.when((turn == 1) == hands_up)
+        def _():
+            for i in (2, 0, 1):
+                upper(i)
+
+        @pl.when(turn == 0)
+        def _():
+            for i in range(3):
+                lower(i)
+
+        return 0
+
+    lax.fori_loop(0, 2, sides, 0)
+
+    @pl.when(~leader)
+    def _():
+        outward[0].wait_recv()
+
+    sums[...] = done[...]
+
+    @pl.when(leader)
+    def _():
+        gathered.wait_send()
+
+    pair = hands_up | hands_down
+    sent(main, pair, xh)
+    sent(main, ~pair, xlo)
+    sent(hand_k, relays, q.at[:, 0, own])
 
 
 def put(count, den, mom, en, sums, ghost, cells, out_d, out_m, out_e, totals, edge, mean, sem):

time: 16.7 us -> 16.7 us (level)
  no operation moved by 1% of the time
where the time goes in v6:
time: 16.7 us; the launch traced here: 16.5 us
  Pallas kernels  15.9 us (95%)
  between operations  0.64 us (4%)
    pallas_call x1, Pallas kernels, shards(): pl.pallas_call(functools.partial(kernel, sizes), out_shape=outputs + tupl...  14.8 us
    pallas_call x1, Pallas kernels, shards(): pl.pallas_call(functools.partial(put, count), out_shape=outputs + (jax.Sh...  1.08 us

profile of v6, /device:TPU:5, one launch (start us, length us, event | category | flops | bytes accessed | tf_op | source)
XLA Modules:
  0.0 16.5 jit_solution(13508916724533966265)
XLA Ops:
  0.6 14.8 %shard_map.84 = (f32[8,64,128]{2,1,0:T(8,128)S(1)}, f32[3,8,64,128]{3,2,1,0:T(8,128)S(1)}, f32[8,64,128]{2,1,0:T(8,128)S(1)}, f32[2,128]{1,0:T(2,128)S(1)}, f32[...) custom-call(s32[6]{0:T(128)} %flags_in.1, f32[8,64,128]{2,1,0:T(8,128)} %den.1, f32[3,8,64,128]{3,2,1,0:T(8,128)} %mom.1, ...), custom_call_target="tpu_custom_call" | custom-call | tf_op jit(solution)/shard_map/pallas_call | solution.py:617
  15.4 1.1 %shard_map.85 = (f32[8,64,128]{2,1,0:T(8,128)}, f32[3,8,64,128]{3,2,1,0:T(8,128)}, f32[8,64,128]{2,1,0:T(8,128)}, f32[2]{0:T(128)}) custom-call(f32[8,64,128]{2,1,0:T(8,128)S(1)} %get-tuple-element.10.den, f32[3,8,64,128]{3,2,1,0:T(8,128)S(1)} %get-tuple-element.11.mom, f32[8,64,128]{2,1,0:T(8,128)S(1)} %get-tuple-element.12.en, ...), custom_call_target="tpu_custom_call" | custom-call | tf_op jit(solution)/shard_map/pallas_call | solution.py:646

commit v7 on v5

--- a/solution.py
+++ b/solution.py
@@ -137,7 +137,7 @@
     hands_up, hands_down = odd & above_x, inner
     relays = (odd & (me >= 3)) | (even & over)
     beside = 1 - 2 * par
-    main, hand_k = 0, 1
+    main, hand_k, last_k = 0, 1, 5
 
     groups = (slice(3, 5), slice(1, 3), 0)
     tops, bottoms = slice(nx - 2, nx), slice(0, 2)
@@ -155,24 +155,30 @@
     up = [piece(main, i, tops, xlo, 0, 1) for i in range(3)]
     down = [piece(main, i, bottoms, xhi, 3, -1) for i in range(3)]
     v_down = copy(2, 6, dx.at[0], xv, "gx", -1)
-    up_across = [piece(main, 0, tops, xlo, 0, 1), one(main, 2, nx - 1, xlo, 1, 1)]
+    keep = ny - SUB
+    far, far_last = slice(0, keep), slice(keep, ny)
+    up_across = [
+        piece(main, 0, tops, xlo, 0, 1),
+        one(main, 2, nx - 1, xlo, 1, 1),
+        copy(main, 1, q.at[0, nx - 2, SUB + keep : top], ghost.at[0, far_last], "gx", 1),
+    ]
     down_across = [piece(main, 0, bottoms, xhi, 3, -1), one(main, 5, 1, xhi, 1, -1)]
     legs_up = [
         copy(main, 7, q.at[1:3, tops, own], hop.at[0:2], "gx", 2),
-        copy(main, 7, q.at[0, nx - 2, own], hop.at[2, 0], "gx", 2),
+        copy(main, 4, q.at[0, nx - 2, SUB : SUB + keep], hop.at[2, 0, far], "gx", 2),
     ]
     legs_down = [
         copy(main, 7, q.at[1:3, bottoms, own], hop.at[0:2], "gx", -2),
         copy(main, 7, q.at[0, 0, own], hop.at[2, 0], "gx", -2),
     ]
 
-    def handed(side):
+    def handed(side, rows):
         return [
             copy(hand_k, 8, hop.at[0:2], side.at[1:3], "gx", beside),
-            copy(hand_k, 9, hop.at[2, 0], dst(side, 0).at[0], "gx", beside),
+            copy(last_k, 9, hop.at[2, 0, rows], dst(side, 0).at[0, rows], "gx", beside),
         ]
 
-    handed_up, handed_down = handed(xlo), handed(xhi)
+    handed_up, handed_down = handed(xlo, far), handed(xhi, slice(0, ny))
 
     def each(cond, copies, act):
         @pl.when(cond)
@@ -190,8 +196,8 @@
         copy(4, 12, dy.at[:, SUB : 2 * SUB], dy.at[:, hi_rows], "gy", -1),
     ]
     both = sz > 2
-    z_up = [copy(5, 13, edge, zlo, "gz", 1)]
-    z_down = [copy(5 + both, 13 + both, edge, zhi, "gz", -1)]
+    z_up = [copy(6, 13, edge, zlo, "gz", 1)]
+    z_down = [copy(6 + both, 13 + both, edge, zhi, "gz", -1)]
 
     def arrive(axis, ups, downs, fill_low, fill_high):
         @pl.when(pos[axis] > 0)
@@ -416,7 +422,9 @@
     pl.when(leader & below_y)(gather)
     lax.fori_loop(early, nx, along_z, 0)
 
-    @pl.when(relays)
+    each(relays & odd, legs_up, lambda c: c.wait_recv())
+
+    @pl.when(relays & even)
     def _():
         copy(hand_k, 7, q.at[:, 0, own], q.at[:, 0, own], "gx", beside).wait_recv()
 
@@ -504,7 +512,7 @@
 
     def lower(i):
         come(odd, [up[i]])
-        come(hands_down, ([up_across[0]], handed_up[:1], [up_across[1], handed_up[1]])[i])
+        come(hands_down, ([up_across[0]], handed_up[:1], up_across[1:] + handed_up[1:])[i])
         if i < 2:
             rims(False, i)
 
@@ -556,13 +564,14 @@
     pair = hands_up | hands_down
     sent(main, pair, xh)
     sent(main, ~pair, xlo)
-    sent(hand_k, relays, q.at[:, 0, own])
+    each(relays & odd, handed_up, lambda c: c.wait_send())
+    each(relays & even, handed_down, lambda c: c.wait_send())
     sent(2, below_x, xv)
     sent(3, above_y & below_y, q.at[:, :, 0 : 2 * SUB])
     sent(3, above_y ^ below_y, q.at[:, :, 0:SUB])
     sent(4, below_y, dy.at[:, 0:SUB])
-    sent(5, above_z, edge)
-    sent(5 + both, below_z, edge)
+    sent(6, above_z, edge)
+    sent(6 + both, below_z, edge)
 
 
 def put(count, den, mom, en, sums, ghost, cells, out_d, out_m, out_e, totals, edge, mean, sem):
@@ -632,7 +641,7 @@
         + [pltpu.VMEM((parts, ny, nz), f32) for _ in range(5)]
         + [pltpu.VMEM((2, nz), f32), pltpu.VMEM((sizes["gx"] * sizes["gz"], 2, nz), f32)]
         + [pltpu.VMEM((sizes["gy"], 2, nz), f32), pltpu.VMEM((2, nz), f32)]
-        + [dma((6 + (sizes["gz"] > 2),)), dma((14 + (sizes["gz"] > 2),)), pltpu.SemaphoreType.REGULAR((4,)), dma((2,)), dma((2,))],
+        + [dma((7 + (sizes["gz"] > 2),)), dma((14 + (sizes["gz"] > 2),)), pltpu.SemaphoreType.REGULAR((4,)), dma((2,)), dma((2,))],
         compiler_params=pltpu.CompilerParams(
             collective_id=0, has_side_effects=True, vmem_limit_bytes=12 << 20
         ),

time: 16.7 us -> 16.6 us (level)
  no operation moved by 1% of the time
where the time goes in v7:
time: 16.6 us; the launch traced here: 16.5 us
  Pallas kernels  15.8 us (95%)
  between operations  0.64 us (4%)
    pallas_call x1, Pallas kernels, shards(): pl.pallas_call(functools.partial(kernel, sizes), out_shape=outputs + tupl...  14.7 us
    pallas_call x1, Pallas kernels, shards(): pl.pallas_call(functools.partial(put, count), out_shape=outputs + (jax.Sh...  1.08 us

profile of v7, /device:TPU:5, one launch (start us, length us, event | category | flops | bytes accessed | tf_op | source)
XLA Modules:
  0.0 16.5 jit_solution(11847980603651678507)
XLA Ops:
  0.6 14.7 %shard_map.84 = (f32[8,64,128]{2,1,0:T(8,128)S(1)}, f32[3,8,64,128]{3,2,1,0:T(8,128)S(1)}, f32[8,64,128]{2,1,0:T(8,128)S(1)}, f32[2,128]{1,0:T(2,128)S(1)}, f32[...) custom-call(s32[6]{0:T(128)} %flags_in.1, f32[8,64,128]{2,1,0:T(8,128)} %den.1, f32[3,8,64,128]{3,2,1,0:T(8,128)} %mom.1, ...), custom_call_target="tpu_custom_call" | custom-call | tf_op jit(solution)/shard_map/pallas_call | solution.py:625
  15.4 1.1 %shard_map.85 = (f32[8,64,128]{2,1,0:T(8,128)}, f32[3,8,64,128]{3,2,1,0:T(8,128)}, f32[8,64,128]{2,1,0:T(8,128)}, f32[2]{0:T(128)}) custom-call(f32[8,64,128]{2,1,0:T(8,128)S(1)} %get-tuple-element.10.den, f32[3,8,64,128]{3,2,1,0:T(8,128)S(1)} %get-tuple-element.11.mom, f32[8,64,128]{2,1,0:T(8,128)S(1)} %get-tuple-element.12.en, ...), custom_call_target="tpu_custom_call" | custom-call | tf_op jit(solution)/shard_map/pallas_call | solution.py:654

commit v8 on v7

--- a/solution.py
+++ b/solution.py
@@ -529,49 +529,50 @@
 
     pl.when(leader)(finish)
 
-    def sides(turn, _):
-        @pl.when((turn == 1) == hands_up)
-        def _():
-            for i in (2, 0, 1):
-                upper(i)
-
-        @pl.when(turn == 0)
-        def _():
-            for i in range(3):
-                lower(i)
-
-        return 0
-
-    lax.fori_loop(0, 2, sides, 0)
-
-    @pl.when(~leader)
-    def _():
-        outward[0].wait_recv()
-        inward.wait_send()
-
-    sums[...] = done[...]
-
-    @pl.when(leader)
-    def _():
-        crossed.wait_send()
-        gathered.wait_send()
-
     def sent(k, cond, ref):
         @pl.when(cond)
         def _():
             copy(k, 0, ref, ref, "gx", beside).wait_send()
 
-    pair = hands_up | hands_down
-    sent(main, pair, xh)
-    sent(main, ~pair, xlo)
-    each(relays & odd, handed_up, lambda c: c.wait_send())
-    each(relays & even, handed_down, lambda c: c.wait_send())
     sent(2, below_x, xv)
     sent(3, above_y & below_y, q.at[:, :, 0 : 2 * SUB])
     sent(3, above_y ^ below_y, q.at[:, :, 0:SUB])
     sent(4, below_y, dy.at[:, 0:SUB])
     sent(6, above_z, edge)
     sent(6 + both, below_z, edge)
+    each(~leader, [inward], lambda c: c.wait_send())
+    each(leader, [crossed], lambda c: c.wait_send())
+
+    def sides(turn, _):
+        @pl.when((turn == 1) == hands_up)
+        def _():
+            for i in (2, 0, 1):
+                upper(i)
+
+        @pl.when(turn == 0)
+        def _():
+            for i in range(3):
+                lower(i)
+
+        return 0
+
+    lax.fori_loop(0, 2, sides, 0)
+
+    @pl.when(~leader)
+    def _():
+        outward[0].wait_recv()
+
+    sums[...] = done[...]
+
+    @pl.when(leader)
+    def _():
+        gathered.wait_send()
+
+    pair = hands_up | hands_down
+    sent(main, pair, xh)
+    sent(main, ~pair, xlo)
+    each(relays & odd, handed_up, lambda c: c.wait_send())
+    each(relays & even, handed_down, lambda c: c.wait_send())
 
 
 def put(count, den, mom, en, sums, ghost, cells, out_d, out_m, out_e, totals, edge, mean, sem):

time: 16.6 us -> 16.6 us (level)
  no operation moved by 1% of the time
where the time goes in v8:
time: 16.6 us; the launch traced here: 16.4 us
  Pallas kernels  15.8 us (95%)
  between operations  0.64 us (4%)
    pallas_call x1, Pallas kernels, shards(): pl.pallas_call(functools.partial(kernel, sizes), out_shape=outputs + tupl...  14.7 us
    pallas_call x1, Pallas kernels, shards(): pl.pallas_call(functools.partial(put, count), out_shape=outputs + (jax.Sh...  1.08 us

profile of v8, /device:TPU:5, one launch (start us, length us, event | category | flops | bytes accessed | tf_op | source)
XLA Modules:
  0.0 16.4 jit_solution(16691305259678949940)
XLA Ops:
  0.6 14.7 %shard_map.84 = (f32[8,64,128]{2,1,0:T(8,128)S(1)}, f32[3,8,64,128]{3,2,1,0:T(8,128)S(1)}, f32[8,64,128]{2,1,0:T(8,128)S(1)}, f32[2,128]{1,0:T(2,128)S(1)}, f32[...) custom-call(s32[6]{0:T(128)} %flags_in.1, f32[8,64,128]{2,1,0:T(8,128)} %den.1, f32[3,8,64,128]{3,2,1,0:T(8,128)} %mom.1, ...), custom_call_target="tpu_custom_call" | custom-call | tf_op jit(solution)/shard_map/pallas_call | solution.py:626
  15.4 1.1 %shard_map.85 = (f32[8,64,128]{2,1,0:T(8,128)}, f32[3,8,64,128]{3,2,1,0:T(8,128)}, f32[8,64,128]{2,1,0:T(8,128)}, f32[2]{0:T(128)}) custom-call(f32[8,64,128]{2,1,0:T(8,128)S(1)} %get-tuple-element.10.den, f32[3,8,64,128]{3,2,1,0:T(8,128)S(1)} %get-tuple-element.11.mom, f32[8,64,128]{2,1,0:T(8,128)S(1)} %get-tuple-element.12.en, ...), custom_call_target="tpu_custom_call" | custom-call | tf_op jit(solution)/shard_map/pallas_call | solution.py:655
